TPU v7x, 256 devices: a whole 4x4x8 slice. The times are simulated.
256 devices in a mesh: seq: 32 (over y, x, core), tensor: 8 (over z).
Axes of the slice: x: 4, y: 4, z: 8, core: 2. Of those that a mesh axis runs over, the one named last changes fastest.
Arguments:
- streams: float32 [4, 16384, 4096], P(None, 'seq', 'tensor'), may hold values from -8 to 8
- mix_weight: float32 [24, 4, 4096], P(None, None, 'tensor'), may hold values from -0.046875 to 0.046875
- mix_bias: float32 [24], replicated, may hold values from -4 to 4
- mix_scale: float32 [3], replicated, may hold values from 1 to 2
- norm_gain: bfloat16 [4096], replicated, may hold values from 0.25 to 1.75
- gate_weight: bfloat16 [4096, 7168], P('seq', 'tensor'), may hold values from -0.09375 to 0.09375
- up_weight: bfloat16 [4096, 7168], P('seq', 'tensor'), may hold values from -0.09375 to 0.09375
- down_weight: bfloat16 [7168, 4096], P('tensor', 'seq'), may hold values from -0.0625 to 0.0625
Outputs:
- new_streams: float32 [4, 16384, 4096], P(None, 'seq', 'tensor')
All inputs are finite; a program needn't handle non-finite values.
Results may differ from a plain program's by a relative error of at most 0.01.
Values may be sent and summed in bfloat16 or wider, within the bound.
A program may use at most 128 MiB of HBM per device.

v0:
```python
import jax
import jax.numpy as jnp
from jax import lax
from jax.sharding import PartitionSpec as P

D = 4096
STREAMS = 4
SWEEPS = 20


epsilon = 0.25


def sent_to_all(shard, axis):
    devices = lax.axis_size(axis)
    return lax.all_to_all(
        jnp.broadcast_to(shard[None], (devices, *shard.shape)), axis, 0, 0, tiled=True
    )


def over_copies(shard, axis):
    everything = sent_to_all(shard, axis)
    return jnp.sum(everything.astype(jnp.float32), axis=0)


def in_order(pieces, dim):
    pieces = jnp.moveaxis(pieces, 0, dim)
    lengths = pieces.shape
    return pieces.reshape(*lengths[:dim], lengths[dim] * lengths[dim + 1], *lengths[dim + 2 :])


def gathered_copies(shard, axis, dim):
    pieces = sent_to_all(shard, axis)
    return in_order(pieces, dim)


def sent_together(arrays, axis, dim, along):
    widths = [a.shape[along] for a in arrays]
    both = jnp.concatenate(arrays, axis=along)
    whole = lax.all_gather(both, axis, axis=dim, tiled=True)
    return tuple(jnp.split(whole, [sum(widths[:k]) for k in range(1, len(widths))], axis=along))


def coefficients(logits, mix_bias, mix_scale):
    pre_mix = jax.nn.sigmoid(mix_scale[0] * logits[:STREAMS] + mix_bias[:STREAMS, None])
    post_mix = 2.0 * jax.nn.sigmoid(
        mix_scale[1] * logits[STREAMS : 2 * STREAMS] + mix_bias[STREAMS : 2 * STREAMS, None]
    )
    start_mix = jnp.exp(mix_scale[2] * logits[2 * STREAMS :] + mix_bias[2 * STREAMS :, None])
    start_mix = start_mix.reshape(STREAMS, STREAMS, logits.shape[1])

    def balance(iteration, matrix):
        matrix = matrix / jnp.sum(matrix, axis=1, keepdims=True)
        return matrix / jnp.sum(matrix, axis=0, keepdims=True)

    return (pre_mix, post_mix, lax.fori_loop(0, SWEEPS, balance, start_mix))


def project_logits(mix_weight, values):
    return jnp.einsum("lkd,ktd->lt", mix_weight, values)


def add_rows(normed, segment):
    return jnp.dot(normed, segment, preferred_element_type=jnp.float32)


def body(streams, mix_weight, mix_bias, mix_scale, norm_gain, gate_weight, up_weight, down_weight):
    feature_count = STREAMS * D
    squares = jnp.sum(streams * streams, axis=(0, 2))[None, :]
    raw_logits = project_logits(mix_weight, streams)
    totals, raw_sums = (
        over_copies(squares.astype(jnp.bfloat16), "tensor").astype(jnp.float32),
        over_copies(raw_logits.astype(jnp.bfloat16), "tensor").astype(jnp.float32),
    )
    logits = raw_sums * lax.rsqrt(totals / feature_count + epsilon)
    pre_mix, post_mix, res_mix = coefficients(logits, mix_bias, mix_scale)
    layer_in = jnp.sum(pre_mix[:, :, None] * streams, axis=0).astype(jnp.bfloat16)
    whole_input = gathered_copies(layer_in, "tensor", 1)
    as_float = whole_input.astype(jnp.float32)
    mean_square = jnp.mean(as_float * as_float, axis=1, keepdims=True)
    normed = (as_float * lax.rsqrt(mean_square + epsilon) * norm_gain.astype(jnp.float32)).astype(
        jnp.bfloat16
    )
    segments = sent_together((gate_weight, up_weight), "seq", 0, 1)
    gate_value = add_rows(normed, segments[0])
    up_value = add_rows(normed, segments[1])
    hidden = (jax.nn.silu(gate_value) * up_value).astype(jnp.bfloat16)
    partial_out = jnp.dot(
        hidden,
        lax.all_gather(down_weight, "seq", axis=1, tiled=True),
        preferred_element_type=jnp.float32,
    )
    layer_out = lax.psum_scatter(
        partial_out.astype(jnp.bfloat16), "tensor", scatter_dimension=1, tiled=True
    ).astype(jnp.float32)
    outputs = []
    for target in range(STREAMS):
        mixed = post_mix[target][:, None] * layer_out
        for source in range(STREAMS):
            mixed = mixed + res_mix[target, source][:, None] * streams[source]
        outputs.append(mixed)
    return jnp.stack(outputs)


def solution(mesh):
    placed = (
        P(None, "seq", "tensor"),
        P(None, None, "tensor"),
        P(),
        P(),
        P(),
        P("seq", "tensor"),
        P("seq", "tensor"),
        P("tensor", "seq"),
    )
    return jax.shard_map(
        body, mesh=mesh, in_specs=placed, out_specs=P(None, "seq", "tensor"), check_vma=False
    )
```

profile of v0, /device:TPU:1, one launch (start us, length us, event | category | flops | bytes accessed | tf_op | source)
XLA Modules:
  0.0 248.1 jit_solution(5382124460439812924)
XLA Ops:
  6.5 1.9 pad_maximum_fusion.1
  8.5 0.7 all-gather.5.cloned.1.call-update
  9.2 2.5 %multiply_reduce_fusion.2 = bf16[512]{0:T(512)(128)(2,1)S(1)} fusion(f32[4,512,512]{2,1,0:T(8,128)} %param.10), kind=kLoop, calls=%fused_computation.13 | loop fusion | flops 2096640 | bytes 4195328 | tf_op jit(solution)/shard_map/reduce_sum | solution.py:69
  11.8 0.5 broadcast.40
  12.3 0.7 reduce.3
  13.0 0.6 reshape.64
  13.6 9.0 %all-to-all-start.1 = ((bf16[8,2,256]{2,1,0:T(2,128)(2,1)}), bf16[8,2,256]{2,1,0:T(2,128)(2,1)S(1)}, u32[]{:S(2)}, u32[]{:S(2)}) async-start(bf16[8,2,256]{2,1,0:T(2,128)(2,1)} %reshape.64), calls=%async_computation.1 | async-start | bytes 16384 | tf_op jit(solution)/shard_map/all_to_all | solution.py:16
  22.6 2.9 %fusion.10 = bf16[24,512]{1,0:T(8,128)(2,1)S(1)} fusion(f32[4,512,512]{2,1,0:T(8,128)} %param.10, f32[24,4,512]{2,1,0:T(4,128)S(1)} %copy-done.2), kind=kOutput, calls=%fused_computation.20 | convolution fusion | flops 50331648 | bytes 4415488 | tf_op jit(solution)/shard_map/lkd,ktd->lt/dot_general | solution.py:60
  25.6 3.6 %all-to-all-done.1 = bf16[8,2,256]{2,1,0:T(2,128)(2,1)S(1)} async-done(((bf16[8,2,256]{2,1,0:T(2,128)(2,1)}), bf16[8,2,256]{2,1,0:T(2,128)(2,1)S(1)}, u32[]{:S(2)}, u32[]{:S(2)}) %all-to-all-start.1) | async-done | bytes 8224 | tf_op jit(solution)/shard_map/all_to_all | solution.py:16
  29.2 0.7 broadcast_in_dim.6
  29.9 3.4 %all-to-all-start = ((bf16[8,24,512]{2,1,0:T(8,128)(2,1)}), bf16[8,24,512]{2,1,0:T(8,128)(2,1)S(1)}, u32[]{:S(2)}, u32[]{:S(2)}) async-start(bf16[8,24,512]{2,1,0:T(8,128)(2,1)} %broadcast_in_dim.6), calls=%async_computation | async-start | bytes 393216 | tf_op jit(solution)/shard_map/all_to_all | solution.py:16
  33.3 0.7 fusion.49
  34.0 7.9 %all-to-all-done = bf16[8,24,512]{2,1,0:T(8,128)(2,1)S(1)} async-done(((bf16[8,24,512]{2,1,0:T(8,128)(2,1)}), bf16[8,24,512]{2,1,0:T(8,128)(2,1)S(1)}, u32[]{:S(2)}, u32[]{:S(2)}) %all-to-all-start) | async-done | bytes 196640 | tf_op jit(solution)/shard_map/all_to_all | solution.py:16
  41.9 1.4 fusion.45
  43.3 2.6 %multiply_reduce_fusion.1 = bf16[512,512]{1,0:T(8,128)(2,1)S(1)} fusion(f32[4,512,512]{2,1,0:T(8,128)} %param.10, f32[4,512]{1,0:T(4,128)S(1)} %get-tuple-element.27), kind=kLoop, calls=%fused_computation.12 | loop fusion | flops 1835008 | bytes 4726784 | tf_op jit(solution)/shard_map/reduce_sum | solution.py:77
  45.9 0.2 copy.20
  46.1 2.4 broadcast_in_dim.8
  48.5 4.7 %all-to-all-start.2 = ((bf16[8,512,512]{1,2,0:T(8,128)(2,1)}), bf16[8,512,512]{1,2,0:T(8,128)(2,1)}, u32[]{:S(2)}, u32[]{:S(2)}) async-start(bf16[8,512,512]{1,2,0:T(8,128)(2,1)} %broadcast_in_dim.8), calls=%async_computation.2 | async-start | bytes 8388608 | tf_op jit(solution)/shard_map/all_to_all | solution.py:16
  53.2 0.2 reduce-scatter.2.cloned.1.call-start
  53.5 91.7 %all-to-all-done.2 = bf16[8,512,512]{1,2,0:T(8,128)(2,1)} async-done(((bf16[8,512,512]{1,2,0:T(8,128)(2,1)}), bf16[8,512,512]{1,2,0:T(8,128)(2,1)}, u32[]{:S(2)}, u32[]{:S(2)}) %all-to-all-start.2) | async-done | bytes 4194336 | tf_op jit(solution)/shard_map/all_to_all | solution.py:16
  145.2 3.2 %multiply_reduce_fusion = f32[512]{0:T(512)S(1)} fusion(bf16[8,512,512]{1,2,0:T(8,128)(2,1)} %all-to-all-done.2), kind=kLoop, calls=%fused_computation.5 | loop fusion | flops 6290944 | bytes 4196352 | tf_op jit(solution)/shard_map/reduce_sum | solution.py:80
  148.4 4.1 %fusion.1 = bf16[512,4096]{0,1:T(8,128)(2,1)} fusion(f32[4096]{0:T(1024)S(1)} %convert_element_type.62, f32[512]{0:T(512)S(1)} %add_rsqrt_fusion, bf16[8,512,512]{1,2,0:T(8,128)(2,1)} %all-to-all-done.2), kind=kLoop, calls=%fused_computation.4 | loop fusion | flops 8388608 | bytes 8407040 | tf_op jit(solution)/shard_map/convert_element_type | solution.py:81
  152.5 8.8 %fusion.4 = f32[512,896]{1,0:T(8,128)S(1)} fusion(bf16[512,4096]{0,1:T(8,128)(2,1)} %fusion.1, bf16[4096,1792]{1,0:T(8,128)(2,1)} %all-gather.3.cloned.1.call-done), kind=kOutput, calls=%fused_computation.8 | convolution fusion | flops 3758096384 | bytes 13369344 | tf_op jit(solution)/shard_map/dot_general | solution.py:64
  161.4 16.6 %convolution_convert_fusion = bf16[512,4096]{1,0:T(8,128)(2,1)} fusion(bf16[896,4096]{1,0:T(8,128)(2,1)} %all-gather.5.cloned.1.call-done, f32[512,896]{1,0:T(8,128)S(1)} %fusion.4, bf16[512,4096]{0,1:T(8,128)(2,1)} %fusion.1, bf16[4096,1792]{1,0:T(8,128)(2,1)} %all-gather.3.cloned.1.call-done), kind=kOutput, calls=%fused_computation.10 | convolution fusion | flops 7521042432 | bytes 24903680 | tf_op jit(solution)/shard_map/dot_general | solution.py:88
  178.0 0.7 fusion.34
  178.8 2.1 while.10
  181.0 53.4 %reduce-scatter.2.cloned.1.call-done = bf16[512,512]{1,0:T(8,128)(2,1)} async-done(((bf16[512,4096]{1,0:T(8,128)(2,1)}), bf16[512,512]{1,0:T(8,128)(2,1)}) %reduce-scatter.2.cloned.1.call-update) | async-done | bytes 524304 | tf_op jit(solution)/shard_map/reduce_scatter | solution.py:93
  234.4 2.9 %fusion.25 = (f32[1,512,512]{2,1,0:T(8,128)S(1)}, f32[1,512,512]{2,1,0:T(8,128)S(1)}) fusion(bf16[512,512]{1,0:T(8,128)(2,1)} %reduce-scatter.2.cloned.1.call-done, f32[4,512,512]{2,1,0:T(8,128)} %param.10, f32[512]{0:T(512)S(1)} %bitcast.111, f32[512]{0:T(512)S(1)} %bitcast.112, f32[512]{0:T(512)S(1)} %bitcast.113, f32[512]{0:T(512)S(1)} %bitcast.114, ...), kind=kLoop, calls=%fused_computation.35 | loop fusion | flops 4980736 | bytes 6836224 | tf_op jit(solution)/shard_map/stack | solution.py:102
  237.3 0.7 copy-done
  238.0 0.1 copy-done.1
  238.1 0.9 fusion.15
  239.1 2.5 pad_maximum_fusion
  (89 shorter events, 2.2 us)
Async XLA Ops:
  6.5 16.1 %copy-start.2 = (f32[24,4,512]{2,1,0:T(4,128)S(1)}, f32[24,4,512]{2,1,0:T(4,128)}, u32[]{:S(2)}) copy-start(f32[24,4,512]{2,1,0:T(4,128)} %param.11) | copy-start | bytes 589828
  6.5 146.0 %all-gather.3.cloned.1.call-start = ((), (), s32[]{:S(2)}) async-start(), calls=%async_computation.4 | async-start | bytes 15138816 | tf_op jit(solution)/shard_map/all_gather | solution.py:40
  8.5 152.9 %all-gather.5.cloned.1.call-start = ((), (), s32[]{:S(2)}) async-start(), calls=%async_computation.5 | async-start | bytes 7569408 | tf_op jit(solution)/shard_map/all_gather | solution.py:90
  9.2 16.3 %copy-start.5 = (f32[24]{0:T(128)S(1)}, f32[24]{0:T(128)}, u32[]{:S(2)}) copy-start(f32[24]{0:T(128)} %param.12) | copy-start | bytes 292
  9.2 24.1 %copy-start.4 = (f32[3]{0:T(128)S(1)}, f32[3]{0:T(128)}, u32[]{:S(2)}) copy-start(f32[3]{0:T(128)} %param.13) | copy-start | bytes 40
  13.6 15.6 %all-to-all-start.1 = ((bf16[8,2,256]{2,1,0:T(2,128)(2,1)}), bf16[8,2,256]{2,1,0:T(2,128)(2,1)S(1)}, u32[]{:S(2)}, u32[]{:S(2)}) async-start(bf16[8,2,256]{2,1,0:T(2,128)(2,1)} %reshape.64), calls=%async_computation.1 | async-start | bytes 16384 | tf_op jit(solution)/shard_map/all_to_all | solution.py:16
  29.9 12.0 %all-to-all-start = ((bf16[8,24,512]{2,1,0:T(8,128)(2,1)}), bf16[8,24,512]{2,1,0:T(8,128)(2,1)S(1)}, u32[]{:S(2)}, u32[]{:S(2)}) async-start(bf16[8,24,512]{2,1,0:T(8,128)(2,1)} %broadcast_in_dim.6), calls=%async_computation | async-start | bytes 393216 | tf_op jit(solution)/shard_map/all_to_all | solution.py:16
  48.5 5.0 %copy-start.3 = (bf16[4096]{0:T(1024)(128)(2,1)S(1)}, bf16[4096]{0:T(1024)(128)(2,1)}, u32[]{:S(2)}) copy-start(bf16[4096]{0:T(1024)(128)(2,1)} %param.14) | copy-start | bytes 24580
  48.5 96.7 %all-to-all-start.2 = ((bf16[8,512,512]{1,2,0:T(8,128)(2,1)}), bf16[8,512,512]{1,2,0:T(8,128)(2,1)}, u32[]{:S(2)}, u32[]{:S(2)}) async-start(bf16[8,512,512]{1,2,0:T(8,128)(2,1)} %broadcast_in_dim.8), calls=%async_computation.2 | async-start | bytes 8388608 | tf_op jit(solution)/shard_map/all_to_all | solution.py:16
  53.2 181.2 %reduce-scatter.2.cloned.1.call-start = ((), (), s32[]{:S(2)}) async-start(), calls=%async_computation.6 | async-start | bytes 4718592 | tf_op jit(solution)/shard_map/reduce_scatter | solution.py:93
  234.4 3.6 %copy-start = (f32[4,512,512]{2,1,0:T(8,128)S(1)}, f32[4,512,512]{2,1,0:T(8,128)}, u32[]{:S(2)}) copy-start(f32[4,512,512]{2,1,0:T(8,128)} %param.10) | copy-start | bytes 12582916
  234.4 3.7 %copy-start.1 = (bf16[512,512]{1,0:T(8,128)(2,1)S(1)}, bf16[512,512]{1,0:T(8,128)(2,1)}, u32[]{:S(2)}) copy-start(bf16[512,512]{1,0:T(8,128)(2,1)} %reduce-scatter.2.cloned.1.call-done) | copy-start | bytes 1572868
Sparse Core Ops, SparseCore 0:
  9.9 76.9 all-gather.2
  89.3 60.7 all-gather.4
  178.1 56.2 reduce-scatter.1
where the time goes:
time: 249 us; the launch traced here: 248 us
  waiting for transfers between devices  157 us (63%)
  matrix products  28.2 us (11%)
  other arithmetic  25.2 us (10%)
  starting transfers between devices  17.4 us (7%)
  between operations  13.3 us (5%)
  local copies, waits for them, and re-layouts  6.11 us (2%)
    all_to_all x3, waiting for transfers between devices, sent_to_all(): lax.all_to_all(jnp.broadcast_to(shard[None], (devices, *shard.shape)), ax...  103 us
    reduce_scatter x1, waiting for transfers between devices, body(): lax.psum_scatter(partial_out.astype(jnp.bfloat16), 'tensor', scatter_dime...  53.4 us
    all_to_all x3, starting transfers between devices, sent_to_all(): lax.all_to_all(jnp.broadcast_to(shard[None], (devices, *shard.shape)), ax...  17.1 us
    dot_general x1, matrix products, body(): jnp.dot(hidden, lax.all_gather(down_weight, 'seq', axis=1, tiled=True), p...  16.6 us
    dot_general x1, matrix products, add_rows(): return jnp.dot(normed, segment, preferred_element_type=jnp.float32)  8.79 us
    another operation x3, other arithmetic, body(): return jnp.stack(outputs)  6.29 us
  transfers between devices with their start and end apart: 6, of which 4 were waited for; matrix products, arithmetic and copies ran while one was open for 14% of the time, Pallas kernels for 0%

commit v1 on v0

v1 whole, which is shorter than its diff:
```python
import functools

import jax
import jax.numpy as jnp
from jax import lax
from jax.experimental import pallas as pl
from jax.experimental.pallas import tpu as pltpu
from jax.sharding import PartitionSpec as P

STREAMS = 4
SWEEPS = 20
EPSILON = 0.25
MESH = pl.DeviceIdType.MESH
NX = 4
NY = 4
NZ = 8
TOK = 512
COLS = 512
ROWS = 128
FFL = 896
CHUNKS = 4
CT = TOK // CHUNKS
PERM = (0, 2, 1, 3)
F32 = jnp.float32
BF16 = jnp.bfloat16


def wrap(value, size):
    return lax.rem(value + size, size)


def nt_dot(a, b, precision=None):
    return lax.dot_general(
        a, b, (((1,), (1,)), ((), ())), precision=precision, preferred_element_type=F32
    )


def kernel(
    st_hbm, mw, bias, scale, gain, g_hbm, u_hbm, d_hbm, out_hbm,
    st, wg, wu, wd, xg, hid, rr, rl, sr, sl, pst, ost, sqx, pre_t, coef_t, inv_t, outb, tmp,
    loc_sem, out_sem, w_send, w_recv, ag_send, ag_recv, rs_send, rs_recv,
    ps_send, ps_recv, os_send, os_recv, sq_send, sq_recv,
):
    s = lax.axis_index("seq")
    z = lax.axis_index("tensor")
    core = lax.rem(s, 2)
    x = lax.rem(lax.div(s, 2), NX)
    y = lax.div(s, 2 * NX)

    def at(xx, yy, cc):
        return {"seq": (yy * NX + xx) * 2 + cc, "tensor": z}

    xp, xm = wrap(x + 1, NX), wrap(x - 1, NX)
    yp, ym = wrap(y + 1, NY), wrap(y - 1, NY)
    x_up, x_dn = at(xp, y, core), at(xm, y, core)
    y_up, y_dn = at(x, yp, core), at(x, ym, core)
    other = at(x, y, 1 - core)
    right = {"seq": s, "tensor": wrap(z + 1, NZ)}
    left = {"seq": s, "tensor": wrap(z - 1, NZ)}
    z_peers = {d: {"seq": s, "tensor": wrap(z + d, NZ)} for d in range(1, NZ)}

    st_copies = [
        pltpu.make_async_copy(
            st_hbm.at[:, pl.ds(c * CT, CT), :], st.at[:, pl.ds(c * CT, CT), :], loc_sem.at[c]
        )
        for c in range(CHUNKS)
    ]
    w_copies = [
        pltpu.make_async_copy(src, dst.at[core, y, x], loc_sem.at[CHUNKS + i])
        for i, (src, dst) in enumerate(((g_hbm, wg), (u_hbm, wu), (d_hbm, wd)))
    ]
    for c in w_copies:
        c.start()
    for c in st_copies:
        c.start()

    barrier = pltpu.get_barrier_semaphore()
    peers = [x_up, x_dn, y_up, y_dn, other] + [z_peers[d] for d in range(1, NZ)]
    for peer in peers:
        pl.semaphore_signal(barrier, inc=1, device_id=peer, device_id_type=MESH)
    pl.semaphore_wait(barrier, len(peers))

    sends = []

    def remote(ref, send_sem, recv_sem, dev):
        return pltpu.make_async_remote_copy(
            src_ref=ref, dst_ref=ref, send_sem=send_sem, recv_sem=recv_sem,
            device_id=dev, device_id_type=MESH,
        )

    items = (
        (wg, 0, ROWS, True),
        (wu, 0, ROWS, False),
        (wd, 0, FFL // 2, True),
        (wd, FFL // 2, FFL // 2, False),
    )

    def w_region(i, cc, f, sec, start, count, r0, nr):
        ref, base, rows, x_first = items[i]
        rsl = pl.ds(base + r0, nr)
        if x_first:
            return ref.at[cc, sec, pl.ds(f, count) if count > 1 else f, rsl, :]
        return ref.at[cc, pl.ds(f, count) if count > 1 else f, sec, rsl, :]

    def axes(i):
        if items[i][3]:
            return x, y, x_up, x_dn, y_up, y_dn
        return y, x, y_up, y_dn, x_up, x_dn

    def w_copy(i, k, dev, region):
        return remote(region, w_send.at[i, k], w_recv.at[i, k], dev)

    def w_go(i, k, dev, region):
        c = w_copy(i, k, dev, region)
        c.start()
        sends.append(c)

    def w_got(i, k, region):
        w_copy(i, k, other, region).wait_recv()

    def step1(i):
        f, sec, f_up, f_dn, _, _ = axes(i)
        rows = items[i][2]
        own = w_region(i, core, f, sec, 0, 1, 0, rows)
        w_go(i, 0, f_up, own)
        w_go(i, 1, f_dn, own)

    def step2(i):
        f, sec, f_up, f_dn, _, _ = axes(i)
        rows = items[i][2]
        half = rows // 2
        fm, fp = wrap(f - 1, 4), wrap(f + 1, 4)
        w_got(i, 0, w_region(i, core, fm, sec, 0, 1, 0, rows))
        w_go(i, 2, f_up, w_region(i, core, fm, sec, 0, 1, 0, half))
        w_got(i, 1, w_region(i, core, fp, sec, 0, 1, 0, rows))
        w_go(i, 3, f_dn, w_region(i, core, fp, sec, 0, 1, half, half))

    def row_to_other(i, k, sec):
        w_go(i, k, other, w_region(i, core, 0, sec, 0, 4, 0, items[i][2]))

    def step2_end(i):
        f, sec, _, _, _, _ = axes(i)
        half = items[i][2] // 2
        f2 = wrap(f + 2, 4)
        w_got(i, 2, w_region(i, core, f2, sec, 0, 1, 0, half))
        w_got(i, 3, w_region(i, core, f2, sec, 0, 1, half, half))

    def pair(i, cc, p, sec):
        return w_region(i, cc, 2 * p, sec, 0, 2, 0, items[i][2])

    def step3(i):
        _, sec, _, _, s_up, s_dn = axes(i)
        w_go(i, 4, s_up, pair(i, core, 0, sec))
        w_go(i, 7, s_dn, pair(i, core, 1, sec))
        w_go(i, 5, s_up, pair(i, core, 1, sec))
        w_go(i, 6, s_dn, pair(i, core, 0, sec))

    def step4(i):
        _, sec, _, _, s_up, s_dn = axes(i)
        sm, sp = wrap(sec - 1, 4), wrap(sec + 1, 4)
        w_got(i, 4, pair(i, core, 0, sm))
        w_go(i, 8, s_up, pair(i, core, 0, sm))
        w_got(i, 7, pair(i, core, 1, sp))
        w_go(i, 9, s_dn, pair(i, core, 1, sp))

    def step4_mid(i):
        _, sec, _, _, _, _ = axes(i)
        sm, sp = wrap(sec - 1, 4), wrap(sec + 1, 4)
        w_got(i, 5, pair(i, core, 1, sm))
        row_to_other(i, 11, sm)
        w_got(i, 6, pair(i, core, 0, sp))
        row_to_other(i, 12, sp)

    def step4_end(i):
        _, sec, _, _, _, _ = axes(i)
        s2 = wrap(sec + 2, 4)
        w_got(i, 8, pair(i, core, 0, s2))
        w_got(i, 9, pair(i, core, 1, s2))
        row_to_other(i, 13, s2)

    def others_rows(i):
        _, sec, _, _, _, _ = axes(i)
        for k, sec_k in ((10, sec), (11, wrap(sec - 1, 4)), (12, wrap(sec + 1, 4)), (13, wrap(sec + 2, 4))):
            w_got(i, k, w_region(i, 1 - core, 0, sec_k, 0, 4, 0, items[i][2]))

    def own_row_to_other(i):
        row_to_other(i, 10, axes(i)[1])

    for c in w_copies:
        c.wait()
    for i in range(4):
        step1(i)

    ones = jnp.ones((8, 128), F32)
    for c in range(CHUNKS):
        st_copies[c].wait()
        tok = pl.ds(c * CT, CT)
        squares = jnp.zeros((CT, COLS), F32)
        raw = jnp.zeros((24, CT), F32)
        for k in range(STREAMS):
            v = st[k, tok, :]
            squares = squares + v * v
            raw = raw + nt_dot(mw[:, k, :], v)
        squares = (squares[:, :128] + squares[:, 128:256]) + (squares[:, 256:384] + squares[:, 384:])
        sq_row = nt_dot(ones, squares, lax.Precision.HIGHEST)
        pst[z, 0:4, tok] = raw[0:4]
        pst[z, 4:8, tok] = sq_row[4:8]
        ost[z, 0:20, tok] = raw[4:24]
        ost[z, 20:24, tok] = sq_row[4:8]
    for d in (4, 3, 5, 2, 6, 1, 7):
        c = remote(pst.at[z], ps_send.at[d], ps_recv.at[d], z_peers[d])
        c.start()
        sends.append(c)
    for d in (4, 3, 5, 2, 6, 1, 7):
        c = remote(ost.at[z], os_send.at[d], os_recv.at[d], z_peers[d])
        c.start()
        sends.append(c)
    for d in range(1, NZ):
        remote(pst.at[wrap(z - d, NZ)], ps_send.at[d], ps_recv.at[d], z_peers[d]).wait_recv()

    total = pst[0]
    for o in range(1, NZ):
        total = total + pst[o]
    inverse = lax.rsqrt(total[4:5] / float(STREAMS * COLS * NZ) + EPSILON)
    row8 = lax.broadcasted_iota(jnp.int32, (8, 1), 0)
    bias8 = jnp.zeros((8, 1), F32)
    for l in range(4):
        bias8 = jnp.where(row8 == l, bias[l], bias8)
    pre = jax.nn.sigmoid(scale[0] * (total * inverse) + bias8)
    pre = jnp.concatenate([pre, jnp.zeros((120, TOK), F32)], axis=0)
    pre_t[...] = pre.T

    def hops(c, to_right):
        return 4 if (c % 2 == 0) == to_right else 3

    def ag_copy(c, h, to_right, origin):
        q = 0 if to_right else 1
        return remote(
            xg.at[origin, pl.ds(c * CT, CT), :], ag_send.at[q, c, h], ag_recv.at[q, c, h],
            right if to_right else left,
        )

    def ag_go(c, h, to_right, origin):
        cp = ag_copy(c, h, to_right, origin)
        cp.start()
        sends.append(cp)

    g_row = gain[z]
    for c in range(CHUNKS):
        tok = pl.ds(c * CT, CT)
        layer_in = pre_t[tok, 0:1] * st[0, tok, :]
        for k in range(1, STREAMS):
            layer_in = layer_in + pre_t[tok, k : k + 1] * st[k, tok, :]
        sent = (layer_in * g_row).astype(BF16)
        for q in range(4):
            xg[z, tok, q * 128 : (q + 1) * 128] = sent[:, PERM[q] * 128 : (PERM[q] + 1) * 128]
        ag_go(c, 0, True, z)
        ag_go(c, 0, False, z)
        sq = layer_in * layer_in
        sq = (sq[:, :128] + sq[:, 128:256]) + (sq[:, 256:384] + sq[:, 384:])
        sqx[z, :, tok] = nt_dot(ones, sq, lax.Precision.HIGHEST)[0:1]
    for d in (4, 3, 5, 2, 6, 1, 7):
        c = remote(sqx.at[z], sq_send.at[d], sq_recv.at[d], z_peers[d])
        c.start()
        sends.append(c)

    def ag_step(h):
        for c in range(CHUNKS):
            for to_right in (True, False):
                if h < hops(c, to_right):
                    origin = wrap(z - (h + 1), NZ) if to_right else wrap(z + (h + 1), NZ)
                    ag_copy(c, h, to_right, origin).wait_recv()
                    if h + 1 < hops(c, to_right):
                        ag_go(c, h + 1, to_right, origin)

    for i in range(4):
        step2(i)
    for i in range(2):
        step2_end(i)
        step3(i)
        own_row_to_other(i)
    for i in range(2, 4):
        step2_end(i)
        own_row_to_other(i)

    for d in range(1, NZ):
        remote(ost.at[wrap(z - d, NZ)], os_send.at[d], os_recv.at[d], z_peers[d]).wait_recv()
    rest = ost[0]
    for o in range(1, NZ):
        rest = rest + ost[o]
    rest = rest * inverse
    row4 = lax.broadcasted_iota(jnp.int32, (4, 1), 0)

    def bias4(first):
        b = jnp.full((4, 1), bias[first], F32)
        for l in range(1, 4):
            b = jnp.where(row4 == l, bias[first + l], b)
        return b

    post = 2.0 * jax.nn.sigmoid(scale[1] * rest[0:4] + bias4(4))
    mix = tuple(
        jnp.exp(scale[2] * rest[4 + 4 * k : 8 + 4 * k] + bias4(8 + 4 * k)) for k in range(4)
    )

    def balance(_, m):
        m = tuple(v / jnp.sum(v, axis=0, keepdims=True) for v in m)
        col = (m[0] + m[1]) + (m[2] + m[3])
        return tuple(v / col for v in m)

    mix = lax.fori_loop(0, SWEEPS, balance, mix)
    coef = jnp.concatenate((post,) + mix + (jnp.zeros((108, TOK), F32),), axis=0)
    coef_t[...] = coef.T

    ag_step(0)
    for i in range(2):
        step4(i)
    for i in range(2, 4):
        step3(i)
    ag_step(1)
    for i in range(2):
        step4_mid(i)
    for d in range(1, NZ):
        remote(sqx.at[wrap(z - d, NZ)], sq_send.at[d], sq_recv.at[d], z_peers[d]).wait_recv()
    sq_total = sqx[0]
    for o in range(1, NZ):
        sq_total = sq_total + sqx[o]
    inv = lax.rsqrt(sq_total / float(COLS * NZ) + EPSILON)
    inv_t[...] = jnp.broadcast_to(inv, (128, TOK)).T
    ag_step(2)
    for i in range(2):
        step4_end(i)
    for i in range(2, 4):
        step4(i)
    for i in range(2):
        others_rows(i)
    ag_step(3)

    halves = 2
    ht = TOK // halves
    n_tiles = FFL // 128

    def gate_up(half):
        def tile(n, carry):
            tok = pl.ds(half * ht, ht)
            lanes = pl.ds(pl.multiple_of(n * 128, 128), 128)
            acc = None
            for b in range(NZ):
                for cc in range(2):
                    a = xg[b, tok, cc * 256 : (cc + 1) * 256]
                    j = 2 * (b % 2)
                    bg = wg[cc, b // 2, j : j + 2, :, lanes].reshape(256, 128)
                    bu = wu[cc, b // 2, j : j + 2, :, lanes].reshape(256, 128)
                    d = jnp.dot(a, jnp.concatenate([bg, bu], axis=1), preferred_element_type=F32)
                    acc = d if acc is None else acc + d
            scale_t = inv_t[tok, :]
            g = acc[:, :128] * scale_t
            u = acc[:, 128:] * scale_t
            hid[tok, lanes] = (g / (1.0 + jnp.exp(-g)) * u).astype(BF16)
            return carry

        lax.fori_loop(0, n_tiles, tile, 0)

    gate_up(0)
    for i in range(2, 4):
        step4_mid(i)
    gate_up(1)
    for i in range(2, 4):
        step4_end(i)
    for i in range(2, 4):
        others_rows(i)

    def partial(dest, tok):
        a = hid[tok, :]
        parts = []
        j = 2 * lax.rem(dest, 2)
        for cc in range(2):
            b0 = wd[cc, lax.div(dest, 2), j]
            b1 = wd[cc, lax.div(dest, 2), j + 1]
            parts.append(
                jnp.dot(a, jnp.concatenate([b0, b1], axis=1), preferred_element_type=F32)
            )
        return parts

    def rs_copy(q, c, t):
        src, dst = (sr, rr) if q == 0 else (sl, rl)
        return pltpu.make_async_remote_copy(
            src_ref=src.at[c, t], dst_ref=dst.at[c, t],
            send_sem=rs_send.at[q, c, t], recv_sem=rs_recv.at[q, c, t],
            device_id=right if q == 0 else left, device_id_type=MESH,
        )

    def rs_body(idx, carry):
        t = lax.div(idx, CHUNKS)
        c = lax.rem(idx, CHUNKS)
        odd = lax.rem(c, 2)
        tok = pl.ds(pl.multiple_of(c * CT, CT), CT)
        for q in range(2):
            n_hops = 4 - odd if q == 0 else 3 + odd

            @pl.when(t < n_hops)
            def _():
                dest = wrap(z + n_hops - t, NZ) if q == 0 else wrap(z - n_hops + t, NZ)
                p0, p1 = partial(dest, tok)
                src, dst = (sr, rr) if q == 0 else (sl, rl)

                @pl.when(t == 0)
                def _():
                    src[c, t, :, 0:256] = p0.astype(BF16)
                    src[c, t, :, 256:512] = p1.astype(BF16)

                @pl.when(t > 0)
                def _():
                    tmp[:, 0:256] = p0
                    tmp[:, 256:512] = p1
                    rs_copy(q, c, t - 1).wait_recv()
                    src[c, t] = (tmp[...] + dst[c, t - 1].astype(F32)).astype(BF16)

                rs_copy(q, c, t).start()

        return carry

    lax.fori_loop(0, 4 * CHUNKS, rs_body, 0)

    def out_copy(c):
        tok = pl.ds(pl.multiple_of(c * CT, CT), CT)
        return pltpu.make_async_copy(outb.at[:, tok, :], out_hbm.at[:, tok, :], out_sem.at[c])

    def out_body(c, carry):
        odd = lax.rem(c, 2)
        tok = pl.ds(pl.multiple_of(c * CT, CT), CT)
        p0, p1 = partial(z, tok)
        tmp[:, 0:256] = p0
        tmp[:, 256:512] = p1
        rs_copy(0, c, 3 - odd).wait_recv()
        rs_copy(1, c, 2 + odd).wait_recv()
        tmp[...] = (
            tmp[...] + rr[c, 3 - odd].astype(F32) + rl[c, 2 + odd].astype(F32)
        )
        for k in range(STREAMS):
            for q in range(4):
                lanes = slice(PERM[q] * 128, (PERM[q] + 1) * 128)
                v = coef_t[tok, k : k + 1] * tmp[:, q * 128 : (q + 1) * 128]
                for j in range(STREAMS):
                    col = 4 + 4 * k + j
                    v = v + coef_t[tok, col : col + 1] * st[j, tok, lanes]
                outb[k, tok, lanes] = v
        out_copy(c).start()
        return carry

    lax.fori_loop(0, CHUNKS, out_body, 0)

    for c in sends:
        c.wait_send()

    def drain(idx, carry):
        t = lax.div(idx, CHUNKS)
        c = lax.rem(idx, CHUNKS)
        odd = lax.rem(c, 2)
        for q in range(2):
            n_hops = 4 - odd if q == 0 else 3 + odd

            @pl.when(t < n_hops)
            def _():
                rs_copy(q, c, t).wait_send()

        return carry

    lax.fori_loop(0, 4 * CHUNKS, drain, 0)
    for c in range(CHUNKS):
        out_copy(c).wait()


def body(streams, mix_weight, mix_bias, mix_scale, norm_gain, gate_weight, up_weight, down_weight):
    gain = norm_gain.astype(F32).reshape(NZ, 1, COLS)
    any_space = pl.BlockSpec(memory_space=pl.ANY)
    vmem = pl.BlockSpec(memory_space=pltpu.VMEM)
    smem = pl.BlockSpec(memory_space=pltpu.SMEM)
    dma = pltpu.SemaphoreType.DMA
    call = pl.pallas_call(
        kernel,
        out_shape=jax.ShapeDtypeStruct((STREAMS, TOK, COLS), F32),
        in_specs=[any_space, vmem, smem, smem, vmem, any_space, any_space, any_space],
        out_specs=any_space,
        scratch_shapes=[
            pltpu.VMEM((STREAMS, TOK, COLS), F32),
            pltpu.VMEM((2, NY, NX, ROWS, FFL), BF16),
            pltpu.VMEM((2, NY, NX, ROWS, FFL), BF16),
            pltpu.VMEM((2, NY, NX, FFL, 128), BF16),
            pltpu.VMEM((NZ, TOK, COLS), BF16),
            pltpu.VMEM((TOK, FFL), BF16),
            pltpu.VMEM((CHUNKS, 4, CT, COLS), BF16),
            pltpu.VMEM((CHUNKS, 4, CT, COLS), BF16),
            pltpu.VMEM((CHUNKS, 4, CT, COLS), BF16),
            pltpu.VMEM((CHUNKS, 4, CT, COLS), BF16),
            pltpu.VMEM((NZ, 8, TOK), F32),
            pltpu.VMEM((NZ, 24, TOK), F32),
            pltpu.VMEM((NZ, 1, TOK), F32),
            pltpu.VMEM((TOK, 128), F32),
            pltpu.VMEM((TOK, 128), F32),
            pltpu.VMEM((TOK, 128), F32),
            pltpu.VMEM((STREAMS, TOK, COLS), F32),
            pltpu.VMEM((CT, COLS), F32),
            dma((CHUNKS + 3,)),
            dma((CHUNKS,)),
            dma((4, 14)),
            dma((4, 14)),
            dma((2, CHUNKS, 4)),
            dma((2, CHUNKS, 4)),
            dma((2, CHUNKS, 4)),
            dma((2, CHUNKS, 4)),
            dma((8,)),
            dma((8,)),
            dma((8,)),
            dma((8,)),
            dma((8,)),
            dma((8,)),
        ],
        compiler_params=pltpu.CompilerParams(
            collective_id=0, has_side_effects=True, vmem_limit_bytes=62 * 1024 * 1024
        ),
    )
    return call(
        streams, mix_weight, mix_bias, mix_scale, gain, gate_weight, up_weight, down_weight
    )


def solution(mesh):
    placed = (
        P(None, "seq", "tensor"),
        P(None, None, "tensor"),
        P(),
        P(),
        P(),
        P("seq", "tensor"),
        P("seq", "tensor"),
        P("tensor", "seq"),
    )
    return jax.shard_map(
        body, mesh=mesh, in_specs=placed, out_specs=P(None, "seq", "tensor"), check_vma=False
    )
```

time: 249 us -> 133 us (0.53)
  waiting for transfers between devices: 157 us -> 0 us
  Pallas kernels: 0 us -> 127 us
  matrix products: 28.2 us -> 0 us
  other arithmetic: 25.2 us -> 1.3 us
  starting transfers between devices: 17.4 us -> 0 us
  between operations: 13.3 us -> 0.01 us
    pallas_call x0 -> x1, Pallas kernels: none -> 127 us  [body(): call(streams, mix_weight, mix_bias, mix_scale, gain, gate_weight, up_weig...]
    all_to_all x3 -> x0, waiting for transfers between devices: 103 us -> none  [sent_to_all(): lax.all_to_all(jnp.broadcast_to(shard[None], (devices, *shard.shape)), ax...]
    reduce_scatter x1 -> x0, waiting for transfers between devices: 53.4 us -> none  [body(): lax.psum_scatter(partial_out.astype(jnp.bfloat16), 'tensor', scatter_dime...]
    dot_general x3 -> x0, matrix products: 28.2 us -> none  [the longest x1 16.6 us: body(): jnp.dot(hidden, lax.all_gather(down_weight, 'seq', axis=1, tiled=True), p...]
    all_to_all x3 -> x0, starting transfers between devices: 17.1 us -> none  [sent_to_all(): lax.all_to_all(jnp.broadcast_to(shard[None], (devices, *shard.shape)), ax...]
    reduce_sum x45 -> x0, other arithmetic: 9.56 us -> none  [the longest x1 3.2 us: body(): mean_square = jnp.mean(as_float * as_float, axis=1, keepdims=True)]
    another operation x3 -> x0, other arithmetic: 6.29 us -> none  [body(): return jnp.stack(outputs)]
    convert_element_type x2 -> x0, other arithmetic: 4.15 us -> none  [the longest x1 4.15 us: body(): (as_float * lax.rsqrt(mean_square + epsilon) * norm_gain.astype(jnp.float...]
  transfers between devices with their start and end apart: 6 -> 0, of which waited for: 4 -> 0; matrix products, arithmetic and copies ran while one was open for 14% -> 0% of each run, Pallas kernels for 0% -> 0%
where the time goes in v1:
time: 133 us
  Pallas kernels  127 us (95%)
  local copies, waits for them, and re-layouts  4.64 us (3%)
    pallas_call x1, Pallas kernels, body(): call(streams, mix_weight, mix_bias, mix_scale, gain, gate_weight, up_weig...  127 us
    unnamed x1, local copies, waits for them, and re-layouts  4.64 us

profile of v1, /device:TPU:1, one launch (start us, length us, event | category | flops | bytes accessed | tf_op | source)
XLA Modules:
  0.0 133.1 jit_solution(7235250404313465312)
XLA Ops:
  0.0 1.3 reshape.7
  1.3 127.1 %shard_map.82 = f32[4,512,512]{2,1,0:T(8,128)} custom-call(f32[4,512,512]{2,1,0:T(8,128)} %st_hbm.1, f32[24,4,512]{2,1,0:T(4,128)} %mw.1, f32[24]{0:T(128)} %bias.1, f32[3]{0:T(128)} %scale.1, f32[8,1,512]{2,1,0:T(1,128)} %bitcast.1, bf16[128,896]{1,0:T(8,128)(2,1)} %g_hbm.1, bf16[128,896]{1,0:T(8,128)(2,1)} %u_hbm.1, bf16[896,128]{1,0:T(8,128)(2,1)} %d_hbm.1), custom_call_target="tpu_custom_call" | custom-call | tf_op jit(solution)/shard_map/pallas_call | solution.py:522
  128.4 4.6 %copy.10 = f32[4,512,512]{2,1,0:T(8,128)} copy(f32[4,512,512]{2,1,0:T(8,128)} %shard_map.82) | data formatting | bytes 8388608

commit v2 on v1

v2 whole, which is shorter than its diff:
```python
import functools

import jax
import jax.numpy as jnp
from jax import lax
from jax.experimental import pallas as pl
from jax.experimental.pallas import tpu as pltpu
from jax.sharding import PartitionSpec as P

STREAMS = 4
SWEEPS = 20
EPSILON = 0.25
MESH = pl.DeviceIdType.MESH
NX = 4
NY = 4
NZ = 8
TOK = 512
COLS = 512
ROWS = 128
FFL = 896
CHUNKS = 4
CT = TOK // CHUNKS
PERM = (0, 2, 1, 3)
F32 = jnp.float32
BF16 = jnp.bfloat16


def wrap(value, size):
    return lax.rem(value + size, size)


def nt_dot(a, b, precision=None):
    return lax.dot_general(
        a, b, (((1,), (1,)), ((), ())), precision=precision, preferred_element_type=F32
    )


def kernel(
    st_hbm, mw, bias, scale, gain, g_hbm, u_hbm, d_hbm, lo, coef_t,
    st, wg, wu, wd, xg, hid, rr, rl, sr, sl, pst, ost, sqx, pre_t, inv_t, tmp, g32,
    loc_sem, w_send, w_recv, ag_send, ag_recv, rs_send, rs_recv,
    ps_send, ps_recv, os_send, os_recv, sq_send, sq_recv,
):
    s = lax.axis_index("seq")
    z = lax.axis_index("tensor")
    core = lax.rem(s, 2)
    x = lax.rem(lax.div(s, 2), NX)
    y = lax.div(s, 2 * NX)

    def at(xx, yy, cc):
        return {"seq": (yy * NX + xx) * 2 + cc, "tensor": z}

    x_up, x_dn = at(wrap(x + 1, NX), y, core), at(wrap(x - 1, NX), y, core)
    y_up, y_dn = at(x, wrap(y + 1, NY), core), at(x, wrap(y - 1, NY), core)
    other = at(x, y, 1 - core)
    right = {"seq": s, "tensor": wrap(z + 1, NZ)}
    left = {"seq": s, "tensor": wrap(z - 1, NZ)}
    z_peers = {d: {"seq": s, "tensor": wrap(z + d, NZ)} for d in range(1, NZ)}
    far_first = (4, 3, 5, 2, 6, 1, 7)

    w_copies = [
        pltpu.make_async_copy(src, dst.at[core, y, x], loc_sem.at[CHUNKS + i])
        for i, (src, dst) in enumerate(((g_hbm, wg), (u_hbm, wu), (d_hbm, wd)))
    ]
    st_copies = [
        pltpu.make_async_copy(
            st_hbm.at[:, pl.ds(c * CT, CT), :], st.at[:, pl.ds(c * CT, CT), :], loc_sem.at[c]
        )
        for c in range(CHUNKS)
    ]
    for c in w_copies[:2] + st_copies + w_copies[2:]:
        c.start()

    barrier = pltpu.get_barrier_semaphore()
    peers = [x_up, x_dn, y_up, y_dn, other] + [z_peers[d] for d in range(1, NZ)]
    for peer in peers:
        pl.semaphore_signal(barrier, inc=1, device_id=peer, device_id_type=MESH)
    g32[...] = gain[...].astype(F32)
    pl.semaphore_wait(barrier, len(peers))

    sends = []

    def remote(ref, send_sem, recv_sem, dev):
        return pltpu.make_async_remote_copy(
            src_ref=ref, dst_ref=ref, send_sem=send_sem, recv_sem=recv_sem,
            device_id=dev, device_id_type=MESH,
        )

    GATE, UP, DOWN = 0, 1, 2
    items = ((wg, ROWS, True), (wu, ROWS, False), (wd, FFL, False))

    def axes(i):
        if items[i][2]:
            return x, y, x_up, x_dn, y_up, y_dn
        return y, x, y_up, y_dn, x_up, x_dn

    def shard(i, f, sec, half=None, cc=None):
        ref, rows, x_first = items[i]
        cc = core if cc is None else cc
        rsl = slice(None) if half is None else pl.ds(half * (rows // 2), rows // 2)
        return ref.at[cc, sec, f, rsl, :] if x_first else ref.at[cc, f, sec, rsl, :]

    def w_copy(i, k, dev, region):
        return remote(region, w_send.at[i, k], w_recv.at[i, k], dev)

    def w_go(i, k, dev, region):
        c = w_copy(i, k, dev, region)
        c.start()
        sends.append(c)

    def w_got(i, k, region):
        w_copy(i, k, other, region).wait_recv()

    zq = lax.div(z, 2)
    zo = lax.rem(z, 2)
    need = [wrap(zq + 2, 4), wrap(zq + 1 + 2 * zo, 4), wrap(zq + 3 - 2 * zo, 4), wrap(zq, 4)]

    def order(i):
        f = axes(i)[0]
        if i == DOWN:
            return need
        return [f, wrap(f - 1, 4), wrap(f + 1, 4), wrap(f + 2, 4)]

    def forwards(i):
        if i == DOWN:
            return ((0, None), (2, 0), (3, 0)), ((1, None), (2, 1), (3, 1))
        return ((0, None), (1, None)), ((2, None), (3, None))

    def step1(i):
        f, sec, f_up, f_dn, _, _ = axes(i)
        w_go(i, 0, f_up, shard(i, f, sec))
        w_go(i, 1, f_dn, shard(i, f, sec))

    def step2(i):
        f, sec, f_up, f_dn, _, _ = axes(i)
        fm, fp = wrap(f - 1, 4), wrap(f + 1, 4)
        w_got(i, 0, shard(i, fm, sec))
        w_go(i, 2, f_up, shard(i, fm, sec, 0))
        w_got(i, 1, shard(i, fp, sec))
        w_go(i, 3, f_dn, shard(i, fp, sec, 1))

    def step2_end(i):
        f, sec = axes(i)[:2]
        w_got(i, 2, shard(i, wrap(f + 2, 4), sec, 0))
        w_got(i, 3, shard(i, wrap(f + 2, 4), sec, 1))

    def half_up(r, n):
        k = 4 + r if n == 0 else 30 + r
        w_go(DOWN, k, axes(DOWN)[4], shard(DOWN, need[r], x, n))

    def half_dn(r, n):
        k = 8 + r if n == 1 else 32 + r
        w_go(DOWN, k, axes(DOWN)[5], shard(DOWN, need[r], x, n))

    def got_half_up(r, n):
        w_got(DOWN, 4 + r if n == 0 else 30 + r, shard(DOWN, need[r], wrap(x - 1, 4), n))

    def got_half_dn(r, n):
        w_got(DOWN, 8 + r if n == 1 else 32 + r, shard(DOWN, need[r], wrap(x + 1, 4), n))

    def fwd_half_up(r):
        got_half_up(r, 0)
        w_go(DOWN, 11 + r, axes(DOWN)[4], shard(DOWN, need[r], wrap(x - 1, 4), 0))

    def fwd_half_dn(r):
        got_half_dn(r, 1)
        w_go(DOWN, 14 + r, axes(DOWN)[5], shard(DOWN, need[r], wrap(x + 1, 4), 1))

    def send_halves(r):
        half_up(r, 0)
        half_dn(r, 1)
        half_up(r, 1)
        half_dn(r, 0)

    def across_up(i, r):
        w_go(i, 4 + r, axes(i)[4], shard(i, order(i)[r], axes(i)[1]))

    def across_dn(i, r):
        w_go(i, 8 + r, axes(i)[5], shard(i, order(i)[r], axes(i)[1]))

    def got_up(i, r):
        w_got(i, 4 + r, shard(i, order(i)[r], wrap(axes(i)[1] - 1, 4)))

    def got_dn(i, r):
        w_got(i, 8 + r, shard(i, order(i)[r], wrap(axes(i)[1] + 1, 4)))

    def fwd_up(i, n):
        r, half = forwards(i)[0][n]
        if n == 0 or forwards(i)[0][n - 1][0] != r:
            got_up(i, r)
        w_go(i, 12 + n, axes(i)[4], shard(i, order(i)[r], wrap(axes(i)[1] - 1, 4), half))

    def fwd_dn(i, n):
        r, half = forwards(i)[1][n]
        got_dn(i, r)
        w_go(i, 15 + n, axes(i)[5], shard(i, order(i)[r], wrap(axes(i)[1] + 1, 4), half))

    def got_fwd_up(i, n):
        r, half = forwards(i)[0][n]
        w_got(i, 12 + n, shard(i, order(i)[r], wrap(axes(i)[1] + 2, 4), half))

    def got_fwd_dn(i, n):
        r, half = forwards(i)[1][n]
        w_got(i, 15 + n, shard(i, order(i)[r], wrap(axes(i)[1] + 2, 4), half))

    def share(i, k, region):
        w_go(i, k, other, region(core))

    def shared(i, k, region):
        w_got(i, k, region(1 - core))

    def row(i, n):
        sec = wrap(axes(i)[1] + (0, -1, 1)[n], 4)
        ref = items[i][0]
        return lambda cc: ref.at[cc, sec] if items[i][2] else ref.at[cc, :, sec]

    def single(i, r, step):
        f, sec = order(i)[r], wrap(axes(i)[1] + step, 4)
        return lambda cc: shard(i, f, sec, None, cc)

    def share_row(i, n):
        share(i, 18 + n, row(i, n))

    def share_far(i, r):
        share(i, 21 + r, single(i, r, 2))

    def all_shared(i):
        for n in range(3):
            shared(i, 18 + n, row(i, n))
        for r in (0, 2, 1, 3):
            shared(i, 21 + r, single(i, r, 2))

    def own_down(cc):
        return wd.at[cc, :, x]

    def share_down(r, n):
        share(DOWN, 19 + 3 * r + n, single(DOWN, r, (-1, 1, 2)[n]))

    def down_shared(r):
        for n in range(3):
            shared(DOWN, 19 + 3 * r + n, single(DOWN, r, (-1, 1, 2)[n]))

    for i in (GATE, UP, DOWN):
        w_copies[i].wait()
        step1(i)
    for i in (GATE, UP):
        across_up(i, 0)
        across_dn(i, 0)

    ones = jnp.ones((8, 128), F32)

    def ps_copy(c, d, owner):
        return remote(
            pst.at[owner, :, pl.ds(c * CT, CT)], ps_send.at[c, d], ps_recv.at[c, d], z_peers[d]
        )

    for c in range(CHUNKS):
        st_copies[c].wait()
        tok = pl.ds(c * CT, CT)
        squares = jnp.zeros((CT, COLS), F32)
        raw = jnp.zeros((24, CT), F32)
        for k in range(STREAMS):
            v = st[k, tok, :]
            squares = squares + v * v
            raw = raw + nt_dot(mw[:, k, :], v)
        squares = (squares[:, :128] + squares[:, 128:256]) + (squares[:, 256:384] + squares[:, 384:])
        sq_row = nt_dot(ones, squares, lax.Precision.HIGHEST)
        pst[z, 0:4, tok] = raw[0:4]
        pst[z, 4:8, tok] = sq_row[4:8]
        ost[z, 0:20, tok] = raw[4:24]
        ost[z, 20:24, tok] = sq_row[4:8]
        for d in far_first:
            cp = ps_copy(c, d, z)
            cp.start()
            sends.append(cp)

    def hops(c, to_right):
        return 4 if (c % 2 == 0) == to_right else 3

    def ag_copy(c, h, to_right, origin):
        q = 0 if to_right else 1
        return remote(
            xg.at[origin, pl.ds(c * CT, CT), :], ag_send.at[q, c, h], ag_recv.at[q, c, h],
            right if to_right else left,
        )

    def ag_go(c, h, to_right, origin):
        cp = ag_copy(c, h, to_right, origin)
        cp.start()
        sends.append(cp)

    row8 = lax.broadcasted_iota(jnp.int32, (8, 1), 0)
    bias8 = jnp.zeros((8, 1), F32)
    for l in range(4):
        bias8 = jnp.where(row8 == l, bias[l], bias8)
    g_row = jnp.concatenate([g32[pl.ds(4 * z + q, 1), :] for q in range(4)], axis=1)

    def layer_input(c):
        tok = pl.ds(c * CT, CT)
        for d in far_first:
            ps_copy(c, d, wrap(z - d, NZ)).wait_recv()
        total = pst[0, :, tok]
        for o in range(1, NZ):
            total = total + pst[o, :, tok]
        inverse = lax.rsqrt(total[4:5] / float(STREAMS * COLS * NZ) + EPSILON)
        pre = jax.nn.sigmoid(scale[0] * (total * inverse) + bias8)
        pre = jnp.concatenate([pre, jnp.zeros((120, CT), F32)], axis=0)
        pre_t[tok, :] = pre.T
        layer_in = pre_t[tok, 0:1] * st[0, tok, :]
        for k in range(1, STREAMS):
            layer_in = layer_in + pre_t[tok, k : k + 1] * st[k, tok, :]
        sent = (layer_in * g_row).astype(BF16)
        for q in range(4):
            xg[z, tok, q * 128 : (q + 1) * 128] = sent[:, PERM[q] * 128 : (PERM[q] + 1) * 128]
        ag_go(c, 0, True, z)
        ag_go(c, 0, False, z)
        sq = layer_in * layer_in
        sq = (sq[:, :128] + sq[:, 128:256]) + (sq[:, 256:384] + sq[:, 384:])
        sqx[z, :, tok] = nt_dot(ones, sq, lax.Precision.HIGHEST)[0:1]

    for c in range(CHUNKS):
        layer_input(c)

    def ag_step(h, chunks):
        for c in chunks:
            for to_right in (True, False):
                if h < hops(c, to_right):
                    origin = wrap(z - (h + 1), NZ) if to_right else wrap(z + (h + 1), NZ)
                    ag_copy(c, h, to_right, origin).wait_recv()
                    if h + 1 < hops(c, to_right):
                        ag_go(c, h + 1, to_right, origin)

    for i in (GATE, UP):
        step2(i)
    for i in (UP, GATE):
        across_up(i, 1)
        across_dn(i, 2)
        across_up(i, 2)
        across_dn(i, 1)
    for d in far_first:
        cp = remote(sqx.at[z], sq_send.at[d], sq_recv.at[d], z_peers[d])
        cp.start()
        sends.append(cp)
    ag_step(0, (0, 1))
    step2(DOWN)
    ag_step(0, (2, 3))
    for i in (UP, GATE):
        step2_end(i)
        across_up(i, 3)
        across_dn(i, 3)
        share_row(i, 0)
    ag_step(1, (0, 1))
    fwd_up(UP, 0)
    fwd_up(UP, 1)
    fwd_dn(UP, 0)
    ag_step(1, (2, 3))
    fwd_dn(UP, 1)
    step2_end(DOWN)
    share(DOWN, 18, own_down)
    for up, dn in ((0, 1), (1, 0)):
        across_up(DOWN, up)
        across_dn(DOWN, dn)
    fwd_up(GATE, 0)
    fwd_up(GATE, 1)
    fwd_dn(GATE, 0)
    got_up(UP, 2)
    got_up(UP, 3)
    share_row(UP, 1)
    got_dn(UP, 0)
    got_dn(UP, 1)
    share_row(UP, 2)
    ag_step(2, (0, 1))
    got_fwd_up(UP, 0)
    share_far(UP, 0)
    got_fwd_dn(UP, 0)
    share_far(UP, 2)
    ag_step(2, (2,))
    fwd_dn(GATE, 1)
    got_up(GATE, 2)
    got_up(GATE, 3)
    share_row(GATE, 1)
    got_dn(GATE, 0)
    got_dn(GATE, 1)
    share_row(GATE, 2)
    ag_step(2, (3,))
    for d in far_first:
        cp = remote(ost.at[z], os_send.at[d], os_recv.at[d], z_peers[d])
        cp.start()
        sends.append(cp)
    got_fwd_up(UP, 1)
    share_far(UP, 1)
    got_fwd_dn(UP, 1)
    share_far(UP, 3)
    for d in far_first:
        remote(sqx.at[wrap(z - d, NZ)], sq_send.at[d], sq_recv.at[d], z_peers[d]).wait_recv()
    sq_total = sqx[0]
    for o in range(1, NZ):
        sq_total = sq_total + sqx[o]
    inv = lax.rsqrt(sq_total / float(COLS * NZ) + EPSILON)
    inv_t[...] = jnp.broadcast_to(inv, (128, TOK)).T
    ag_step(3, (0,))
    got_fwd_up(GATE, 0)
    share_far(GATE, 0)
    got_fwd_dn(GATE, 0)
    share_far(GATE, 2)
    fwd_up(DOWN, 0)
    fwd_dn(DOWN, 0)
    send_halves(2)
    share_down(0, 0)
    share_down(1, 1)
    ag_step(3, (1,))
    got_fwd_up(GATE, 1)
    share_far(GATE, 1)
    got_fwd_dn(GATE, 1)
    share_far(GATE, 3)
    all_shared(UP)
    all_shared(GATE)

    halves = 2
    ht = TOK // halves

    def gate_up(half, first, last):
        def tile(n, carry):
            tok = pl.ds(half * ht, ht)
            lanes = pl.ds(pl.multiple_of(n * 128, 128), 128)
            acc = None
            for b in range(NZ):
                for cc in range(2):
                    a = xg[b, tok, cc * 256 : (cc + 1) * 256]
                    j = 2 * (b % 2)
                    bg = wg[cc, b // 2, j : j + 2, :, lanes].reshape(256, 128)
                    bu = wu[cc, b // 2, j : j + 2, :, lanes].reshape(256, 128)
                    d = jnp.dot(a, jnp.concatenate([bg, bu], axis=1), preferred_element_type=F32)
                    acc = d if acc is None else acc + d
            scale_t = inv_t[tok, :]
            g = acc[:, :128] * scale_t
            u = acc[:, 128:] * scale_t
            hid[tok, lanes] = (g / (1.0 + jnp.exp(-g)) * u).astype(BF16)
            return carry

        lax.fori_loop(first, last, tile, 0)

    def partial(dest, tok):
        a = hid[tok, :]
        parts = []
        j = 2 * lax.rem(dest, 2)
        for cc in range(2):
            b0 = wd[cc, lax.div(dest, 2), j]
            b1 = wd[cc, lax.div(dest, 2), j + 1]
            parts.append(
                jnp.dot(a, jnp.concatenate([b0, b1], axis=1), preferred_element_type=F32)
            )
        return parts

    def rs_copy(q, c, t):
        src, dst = (sr, rr) if q == 0 else (sl, rl)
        return pltpu.make_async_remote_copy(
            src_ref=src.at[c, t], dst_ref=dst.at[c, t],
            send_sem=rs_send.at[q, c, t], recv_sem=rs_recv.at[q, c, t],
            device_id=right if q == 0 else left, device_id_type=MESH,
        )

    def rs_step(t, first, last):
        def chunk(c, carry):
            odd = lax.rem(c, 2)
            tok = pl.ds(pl.multiple_of(c * CT, CT), CT)
            for q in range(2):
                n_hops = 4 - odd if q == 0 else 3 + odd

                def send():
                    dest = wrap(z + n_hops - t, NZ) if q == 0 else wrap(z - n_hops + t, NZ)
                    p0, p1 = partial(dest, tok)
                    src, dst = (sr, rr) if q == 0 else (sl, rl)
                    if t == 0:
                        src[c, t, :, 0:256] = p0.astype(BF16)
                        src[c, t, :, 256:512] = p1.astype(BF16)
                    else:
                        tmp[:, 0:256] = p0
                        tmp[:, 256:512] = p1
                        rs_copy(q, c, t - 1).wait_recv()
                        src[c, t] = (tmp[...] + dst[c, t - 1].astype(F32)).astype(BF16)
                    rs_copy(q, c, t).start()

                if t < 3:
                    send()
                else:
                    pl.when(n_hops == 4)(send)
            return carry

        lax.fori_loop(first, last, chunk, 0)

    gate_up(0, 0, 5)
    got_up(DOWN, 1)
    share_down(1, 0)
    got_dn(DOWN, 0)
    share_down(0, 1)
    gate_up(0, 5, 6)
    got_fwd_up(DOWN, 0)
    share_down(0, 2)
    got_fwd_dn(DOWN, 0)
    share_down(1, 2)
    gate_up(0, 6, 7)
    ag_step(3, (2, 3))
    gate_up(1, 0, 1)
    fwd_half_up(2)
    fwd_half_dn(2)
    send_halves(3)
    shared(DOWN, 18, own_down)
    down_shared(0)
    down_shared(1)
    rs_step(0, 0, 2)
    gate_up(1, 1, 4)
    got_half_up(2, 1)
    share_down(2, 0)
    got_half_dn(2, 0)
    share_down(2, 1)
    gate_up(1, 4, 7)
    rs_step(0, 2, 4)
    fwd_half_up(3)
    fwd_half_dn(3)
    got_fwd_up(DOWN, 1)
    got_fwd_dn(DOWN, 1)
    share_down(2, 2)
    down_shared(2)
    rs_step(1, 0, 4)
    got_half_up(3, 1)
    share_down(3, 0)
    got_half_dn(3, 0)
    share_down(3, 1)
    got_fwd_up(DOWN, 2)
    got_fwd_dn(DOWN, 2)
    share_down(3, 2)
    down_shared(3)

    for d in far_first:
        remote(ost.at[wrap(z - d, NZ)], os_send.at[d], os_recv.at[d], z_peers[d]).wait_recv()
    total = pst[0]
    rest = ost[0]
    for o in range(1, NZ):
        total = total + pst[o]
        rest = rest + ost[o]
    rest = rest * lax.rsqrt(total[4:5] / float(STREAMS * COLS * NZ) + EPSILON)
    row4 = lax.broadcasted_iota(jnp.int32, (4, 1), 0)

    def bias4(first):
        b = jnp.full((4, 1), bias[first], F32)
        for l in range(1, 4):
            b = jnp.where(row4 == l, bias[first + l], b)
        return b

    post = 2.0 * jax.nn.sigmoid(scale[1] * rest[0:4] + bias4(4))
    mix = tuple(
        jnp.exp(scale[2] * rest[4 + 4 * k : 8 + 4 * k] + bias4(8 + 4 * k)) for k in range(4)
    )

    def balance(_, m):
        m = tuple(v / jnp.sum(v, axis=0, keepdims=True) for v in m)
        col = (m[0] + m[1]) + (m[2] + m[3])
        return tuple(v / col for v in m)

    mix = lax.fori_loop(0, SWEEPS, balance, mix)
    coef = jnp.concatenate((post,) + mix + (jnp.zeros((108, TOK), F32),), axis=0)
    coef_t[...] = coef.T

    rs_step(2, 0, 4)
    for c in sends:
        c.wait_send()
    rs_step(3, 0, 4)

    def out_body(c, carry):
        odd = lax.rem(c, 2)
        tok = pl.ds(pl.multiple_of(c * CT, CT), CT)
        p0, p1 = partial(z, tok)
        tmp[:, 0:256] = p0
        tmp[:, 256:512] = p1
        rs_copy(0, c, 3 - odd).wait_recv()
        rs_copy(1, c, 2 + odd).wait_recv()
        tmp[...] = (
            tmp[...] + rr[c, 3 - odd].astype(F32) + rl[c, 2 + odd].astype(F32)
        )
        for q in range(4):
            lo[tok, PERM[q] * 128 : (PERM[q] + 1) * 128] = tmp[:, q * 128 : (q + 1) * 128]
        return carry

    lax.fori_loop(0, CHUNKS, out_body, 0)

    for c in range(CHUNKS):
        for q in range(2):
            for t in range(hops(c, q == 0)):
                rs_copy(q, c, t).wait_send()


def mix_kernel(st_hbm, lo_hbm, coef_hbm, out_hbm, st, lo, coef_t, out, in_sem, out_sem):
    def tokens(c):
        return pl.ds(c * CT, CT)

    def reads(c):
        return (
            pltpu.make_async_copy(coef_hbm.at[tokens(c)], coef_t.at[tokens(c)], in_sem.at[c, 0]),
            pltpu.make_async_copy(lo_hbm.at[tokens(c)], lo.at[tokens(c)], in_sem.at[c, 1]),
            pltpu.make_async_copy(st_hbm.at[:, tokens(c)], st.at[:, tokens(c)], in_sem.at[c, 2]),
        )

    def write(c):
        return pltpu.make_async_copy(out.at[:, tokens(c)], out_hbm.at[:, tokens(c)], out_sem.at[c])

    for c in range(CHUNKS):
        for copy in reads(c):
            copy.start()
    rows = 16

    for c in range(CHUNKS):
        for copy in reads(c):
            copy.wait()

        def group(g, carry):
            tok = pl.ds(pl.multiple_of(c * CT + g * rows, rows), rows)
            wide = [
                jnp.broadcast_to(coef_t[tok, n : n + 1], (rows, 128)) for n in range(5 * STREAMS)
            ]
            for q in range(COLS // 128):
                lanes = slice(q * 128, (q + 1) * 128)
                low = lo[tok, lanes]
                src = [st[j, tok, lanes] for j in range(STREAMS)]
                for k in range(STREAMS):
                    v = wide[k] * low
                    for j in range(STREAMS):
                        v = v + wide[STREAMS + STREAMS * k + j] * src[j]
                    out[k, tok, lanes] = v
            return carry

        lax.fori_loop(0, CT // rows, group, 0)
        write(c).start()
    for c in range(CHUNKS):
        write(c).wait()


def body(streams, mix_weight, mix_bias, mix_scale, norm_gain, gate_weight, up_weight, down_weight):
    gain = norm_gain.reshape(NZ * 4, 128)
    hbm = pl.BlockSpec(memory_space=pltpu.HBM)
    vmem = pl.BlockSpec(memory_space=pltpu.VMEM)
    smem = pl.BlockSpec(memory_space=pltpu.SMEM)
    dma = pltpu.SemaphoreType.DMA
    layer_out, coef = pl.pallas_call(
        kernel,
        out_shape=(
            jax.ShapeDtypeStruct((TOK, COLS), F32),
            jax.ShapeDtypeStruct((TOK, 128), F32),
        ),
        in_specs=[hbm, vmem, smem, smem, vmem, hbm, hbm, hbm],
        out_specs=(vmem, vmem),
        scratch_shapes=[
            pltpu.VMEM((STREAMS, TOK, COLS), F32),
            pltpu.VMEM((2, NY, NX, ROWS, FFL), BF16),
            pltpu.VMEM((2, NY, NX, ROWS, FFL), BF16),
            pltpu.VMEM((2, NY, NX, FFL, 128), BF16),
            pltpu.VMEM((NZ, TOK, COLS), BF16),
            pltpu.VMEM((TOK, FFL), BF16),
            pltpu.VMEM((CHUNKS, 4, CT, COLS), BF16),
            pltpu.VMEM((CHUNKS, 4, CT, COLS), BF16),
            pltpu.VMEM((CHUNKS, 4, CT, COLS), BF16),
            pltpu.VMEM((CHUNKS, 4, CT, COLS), BF16),
            pltpu.VMEM((NZ, 8, TOK), F32),
            pltpu.VMEM((NZ, 24, TOK), F32),
            pltpu.VMEM((NZ, 1, TOK), F32),
            pltpu.VMEM((TOK, 128), F32),
            pltpu.VMEM((TOK, 128), F32),
            pltpu.VMEM((CT, COLS), F32),
            pltpu.VMEM((NZ * 4, 128), F32),
            dma((CHUNKS + 3,)),
            dma((3, 36)),
            dma((3, 36)),
            dma((2, CHUNKS, 4)),
            dma((2, CHUNKS, 4)),
            dma((2, CHUNKS, 4)),
            dma((2, CHUNKS, 4)),
            dma((CHUNKS, 8)),
            dma((CHUNKS, 8)),
            dma((8,)),
            dma((8,)),
            dma((8,)),
            dma((8,)),
        ],
        compiler_params=pltpu.CompilerParams(
            collective_id=0, has_side_effects=True, vmem_limit_bytes=60 * 1024 * 1024
        ),
    )(streams, mix_weight, mix_bias, mix_scale, gain, gate_weight, up_weight, down_weight)
    return pl.pallas_call(
        mix_kernel,
        out_shape=jax.ShapeDtypeStruct((STREAMS, TOK, COLS), F32),
        in_specs=[hbm, hbm, hbm],
        out_specs=hbm,
        scratch_shapes=[
            pltpu.VMEM((STREAMS, TOK, COLS), F32),
            pltpu.VMEM((TOK, COLS), F32),
            pltpu.VMEM((TOK, 128), F32),
            pltpu.VMEM((STREAMS, TOK, COLS), F32),
            dma((CHUNKS, 3)),
            dma((CHUNKS,)),
        ],
        compiler_params=pltpu.CompilerParams(vmem_limit_bytes=60 * 1024 * 1024),
    )(streams, layer_out, coef)


def solution(mesh):
    placed = (
        P(None, "seq", "tensor"),
        P(None, None, "tensor"),
        P(),
        P(),
        P(),
        P("seq", "tensor"),
        P("seq", "tensor"),
        P("tensor", "seq"),
    )
    return jax.shard_map(
        body, mesh=mesh, in_specs=placed, out_specs=P(None, "seq", "tensor"), check_vma=False
    )
```

time: 133 us -> 120 us (0.902)
  Pallas kernels: 127 us -> 120 us
  local copies, waits for them, and re-layouts: 4.64 us -> 0 us
    pallas_call x1 -> x2, Pallas kernels: 127 us -> 120 us  [the longest x1 113 us: body(): pl.pallas_call(kernel, out_shape=(jax.ShapeDtypeStruct((TOK, COLS), F32),...]
    unnamed x1 -> x0, local copies, waits for them, and re-layouts: 4.64 us -> none
where the time goes in v2:
time: 120 us
  Pallas kernels  120 us (100%)
    pallas_call x1, Pallas kernels, body(): pl.pallas_call(kernel, out_shape=(jax.ShapeDtypeStruct((TOK, COLS), F32),...  113 us
    pallas_call x1, Pallas kernels, body(): pl.pallas_call(mix_kernel, out_shape=jax.ShapeDtypeStruct((STREAMS, TOK,...  6.77 us

profile of v2, /device:TPU:1, one launch (start us, length us, event | category | flops | bytes accessed | tf_op | source)
XLA Modules:
  0.0 120.2 jit_solution(4735952358270257667)
XLA Ops:
  0.0 113.5 %shard_map.82 = (f32[512,512]{1,0:T(8,128)}, f32[512,128]{1,0:T(8,128)}) custom-call(f32[4,512,512]{2,1,0:T(8,128)} %st_hbm.3, f32[24,4,512]{2,1,0:T(4,128)} %mw.1, f32[24]{0:T(128)} %bias.1, f32[3]{0:T(128)} %scale.1, bf16[32,128]{1,0:T(8,128)(2,1)} %bitcast.1, bf16[128,896]{1,0:T(8,128)(2,1)} %g_hbm.1, bf16[128,896]{1,0:T(8,128)(2,1)} %u_hbm.1, ...), custom_call_target="tpu_custom_call" | custom-call | tf_op jit(solution)/shard_map/pallas_call | solution.py:644
  113.5 6.8 %shard_map.83 = f32[4,512,512]{2,1,0:T(8,128)} custom-call(f32[4,512,512]{2,1,0:T(8,128)} %st_hbm.3, f32[512,512]{1,0:T(8,128)} %get-tuple-element.7.lo_hbm, f32[512,128]{1,0:T(8,128)} %get-tuple-element.8.coef_hbm), custom_call_target="tpu_custom_call" | custom-call | tf_op jit(solution)/shard_map/pallas_call | solution.py:688

commit v3 on v2

--- a/solution.py
+++ b/solution.py
@@ -20,6 +20,7 @@
 FFL = 896
 CHUNKS = 4
 CT = TOK // CHUNKS
+MT = 64
 PERM = (0, 2, 1, 3)
 F32 = jnp.float32
 BF16 = jnp.bfloat16
@@ -36,9 +37,9 @@
 
 
 def kernel(
-    st_hbm, mw, bias, scale, gain, g_hbm, u_hbm, d_hbm, lo, coef_t,
+    st_hbm, mw, bias, scale, gain, g_hbm, u_hbm, d_hbm, base_hbm, lo_hbm, post_hbm,
     st, wg, wu, wd, xg, hid, rr, rl, sr, sl, pst, ost, sqx, pre_t, inv_t, tmp, g32,
-    loc_sem, w_send, w_recv, ag_send, ag_recv, rs_send, rs_recv,
+    base, lo, own, coef_t, loc_sem, out_sem, w_send, w_recv, ag_send, ag_recv, rs_send, rs_recv,
     ps_send, ps_recv, os_send, os_recv, sq_send, sq_recv,
 ):
     s = lax.axis_index("seq")
@@ -68,7 +69,7 @@
         )
         for c in range(CHUNKS)
     ]
-    for c in w_copies[:2] + st_copies + w_copies[2:]:
+    for c in w_copies + st_copies:
         c.start()
 
     barrier = pltpu.get_barrier_semaphore()
@@ -489,26 +490,24 @@
 
         lax.fori_loop(first, last, chunk, 0)
 
-    gate_up(0, 0, 5)
+    gate_up(0, 0, 7)
     got_up(DOWN, 1)
     share_down(1, 0)
     got_dn(DOWN, 0)
     share_down(0, 1)
-    gate_up(0, 5, 6)
+    ag_step(3, (2, 3))
     got_fwd_up(DOWN, 0)
     share_down(0, 2)
     got_fwd_dn(DOWN, 0)
     share_down(1, 2)
-    gate_up(0, 6, 7)
-    ag_step(3, (2, 3))
     gate_up(1, 0, 1)
-    fwd_half_up(2)
-    fwd_half_dn(2)
-    send_halves(3)
     shared(DOWN, 18, own_down)
     down_shared(0)
     down_shared(1)
     rs_step(0, 0, 2)
+    fwd_half_up(2)
+    fwd_half_dn(2)
+    send_halves(3)
     gate_up(1, 1, 4)
     got_half_up(2, 1)
     share_down(2, 0)
@@ -562,24 +561,73 @@
     coef = jnp.concatenate((post,) + mix + (jnp.zeros((108, TOK), F32),), axis=0)
     coef_t[...] = coef.T
 
-    rs_step(2, 0, 4)
+    def post_write():
+        return pltpu.make_async_copy(coef_t, post_hbm, out_sem.at[2 * CHUNKS])
+
+    def base_write(c):
+        tok = pl.ds(pl.multiple_of(c * CT, CT), CT)
+        return pltpu.make_async_copy(base.at[:, tok, :], base_hbm.at[:, tok, :], out_sem.at[c])
+
+    def lo_write(c):
+        tok = pl.ds(pl.multiple_of(c * CT, CT), CT)
+        return pltpu.make_async_copy(lo.at[tok, :], lo_hbm.at[tok, :], out_sem.at[CHUNKS + c])
+
+    def residual(c):
+        rows = 16
+
+        def group(g, carry):
+            tok = pl.ds(pl.multiple_of(c * CT + g * rows, rows), rows)
+            wide = [
+                jnp.broadcast_to(coef_t[tok, STREAMS + n : STREAMS + n + 1], (rows, 128))
+                for n in range(STREAMS * STREAMS)
+            ]
+            for q in range(COLS // 128):
+                lanes = slice(q * 128, (q + 1) * 128)
+                src = [st[j, tok, lanes] for j in range(STREAMS)]
+                for k in range(STREAMS):
+                    v = wide[STREAMS * k] * src[0]
+                    for j in range(1, STREAMS):
+                        v = v + wide[STREAMS * k + j] * src[j]
+                    base[k, tok, lanes] = v
+            return carry
+
+        lax.fori_loop(0, CT // rows, group, 0)
+        base_write(c).start()
+
+    post_write().start()
+    residual(0)
+    rs_step(2, 0, 2)
+    residual(1)
+    rs_step(2, 2, 4)
     for c in sends:
         c.wait_send()
-    rs_step(3, 0, 4)
+    residual(2)
+    rs_step(3, 0, 2)
+    residual(3)
+    rs_step(3, 2, 4)
+
+    def own_body(c, carry):
+        tok = pl.ds(pl.multiple_of(c * CT, CT), CT)
+        p0, p1 = partial(z, tok)
+        own[tok, 0:256] = p0
+        own[tok, 256:512] = p1
+        return carry
+
+    lax.fori_loop(0, CHUNKS, own_body, 0)
 
     def out_body(c, carry):
         odd = lax.rem(c, 2)
         tok = pl.ds(pl.multiple_of(c * CT, CT), CT)
-        p0, p1 = partial(z, tok)
-        tmp[:, 0:256] = p0
-        tmp[:, 256:512] = p1
         rs_copy(0, c, 3 - odd).wait_recv()
         rs_copy(1, c, 2 + odd).wait_recv()
-        tmp[...] = (
-            tmp[...] + rr[c, 3 - odd].astype(F32) + rl[c, 2 + odd].astype(F32)
-        )
         for q in range(4):
-            lo[tok, PERM[q] * 128 : (PERM[q] + 1) * 128] = tmp[:, q * 128 : (q + 1) * 128]
+            lanes = slice(q * 128, (q + 1) * 128)
+            lo[tok, PERM[q] * 128 : (PERM[q] + 1) * 128] = (
+                own[tok, lanes]
+                + rr[c, 3 - odd, :, lanes].astype(F32)
+                + rl[c, 2 + odd, :, lanes].astype(F32)
+            )
+        lo_write(c).start()
         return carry
 
     lax.fori_loop(0, CHUNKS, out_body, 0)
@@ -588,50 +636,37 @@
         for q in range(2):
             for t in range(hops(c, q == 0)):
                 rs_copy(q, c, t).wait_send()
-
-
-def mix_kernel(st_hbm, lo_hbm, coef_hbm, out_hbm, st, lo, coef_t, out, in_sem, out_sem):
+    post_write().wait()
+    for c in range(CHUNKS):
+        base_write(c).wait()
+        lo_write(c).wait()
+
+
+def mix_kernel(base_hbm, lo_hbm, post_hbm, out_hbm, base, lo, post, in_sem, out_sem):
     def tokens(c):
-        return pl.ds(c * CT, CT)
+        return pl.ds(c * MT, MT)
 
     def reads(c):
         return (
-            pltpu.make_async_copy(coef_hbm.at[tokens(c)], coef_t.at[tokens(c)], in_sem.at[c, 0]),
+            pltpu.make_async_copy(post_hbm.at[tokens(c)], post.at[tokens(c)], in_sem.at[c, 0]),
             pltpu.make_async_copy(lo_hbm.at[tokens(c)], lo.at[tokens(c)], in_sem.at[c, 1]),
-            pltpu.make_async_copy(st_hbm.at[:, tokens(c)], st.at[:, tokens(c)], in_sem.at[c, 2]),
+            pltpu.make_async_copy(base_hbm.at[:, tokens(c)], base.at[:, tokens(c)], in_sem.at[c, 2]),
         )
 
     def write(c):
-        return pltpu.make_async_copy(out.at[:, tokens(c)], out_hbm.at[:, tokens(c)], out_sem.at[c])
-
-    for c in range(CHUNKS):
+        return pltpu.make_async_copy(base.at[:, tokens(c)], out_hbm.at[:, tokens(c)], out_sem.at[c])
+
+    for c in range(TOK // MT):
         for copy in reads(c):
             copy.start()
-    rows = 16
-
-    for c in range(CHUNKS):
+    for c in range(TOK // MT):
         for copy in reads(c):
             copy.wait()
-
-        def group(g, carry):
-            tok = pl.ds(pl.multiple_of(c * CT + g * rows, rows), rows)
-            wide = [
-                jnp.broadcast_to(coef_t[tok, n : n + 1], (rows, 128)) for n in range(5 * STREAMS)
-            ]
-            for q in range(COLS // 128):
-                lanes = slice(q * 128, (q + 1) * 128)
-                low = lo[tok, lanes]
-                src = [st[j, tok, lanes] for j in range(STREAMS)]
-                for k in range(STREAMS):
-                    v = wide[k] * low
-                    for j in range(STREAMS):
-                        v = v + wide[STREAMS + STREAMS * k + j] * src[j]
-                    out[k, tok, lanes] = v
-            return carry
-
-        lax.fori_loop(0, CT // rows, group, 0)
+        tok = slice(c * MT, (c + 1) * MT)
+        for k in range(STREAMS):
+            base[k, tok, :] = base[k, tok, :] + post[tok, k : k + 1] * lo[tok, :]
         write(c).start()
-    for c in range(CHUNKS):
+    for c in range(TOK // MT):
         write(c).wait()
 
 
@@ -641,14 +676,15 @@
     vmem = pl.BlockSpec(memory_space=pltpu.VMEM)
     smem = pl.BlockSpec(memory_space=pltpu.SMEM)
     dma = pltpu.SemaphoreType.DMA
-    layer_out, coef = pl.pallas_call(
+    base, layer_out, post = pl.pallas_call(
         kernel,
         out_shape=(
+            jax.ShapeDtypeStruct((STREAMS, TOK, COLS), F32),
             jax.ShapeDtypeStruct((TOK, COLS), F32),
             jax.ShapeDtypeStruct((TOK, 128), F32),
         ),
         in_specs=[hbm, vmem, smem, smem, vmem, hbm, hbm, hbm],
-        out_specs=(vmem, vmem),
+        out_specs=(hbm, hbm, hbm),
         scratch_shapes=[
             pltpu.VMEM((STREAMS, TOK, COLS), F32),
             pltpu.VMEM((2, NY, NX, ROWS, FFL), BF16),
@@ -667,7 +703,12 @@
             pltpu.VMEM((TOK, 128), F32),
             pltpu.VMEM((CT, COLS), F32),
             pltpu.VMEM((NZ * 4, 128), F32),
+            pltpu.VMEM((STREAMS, TOK, COLS), F32),
+            pltpu.VMEM((TOK, COLS), F32),
+            pltpu.VMEM((TOK, COLS), F32),
+            pltpu.VMEM((TOK, 128), F32),
             dma((CHUNKS + 3,)),
+            dma((2 * CHUNKS + 1,)),
             dma((3, 36)),
             dma((3, 36)),
             dma((2, CHUNKS, 4)),
@@ -694,12 +735,11 @@
             pltpu.VMEM((STREAMS, TOK, COLS), F32),
             pltpu.VMEM((TOK, COLS), F32),
             pltpu.VMEM((TOK, 128), F32),
-            pltpu.VMEM((STREAMS, TOK, COLS), F32),
-            dma((CHUNKS, 3)),
-            dma((CHUNKS,)),
+            dma((TOK // MT, 3)),
+            dma((TOK // MT,)),
         ],
         compiler_params=pltpu.CompilerParams(vmem_limit_bytes=60 * 1024 * 1024),
-    )(streams, layer_out, coef)
+    )(base, layer_out, post)
 
 
 def solution(mesh):

time: 120 us -> 119 us (level)
    pallas_call x1, Pallas kernels: 6.77 us -> 4.85 us  [body(): pl.pallas_call(mix_kernel, out_shape=jax.ShapeDtypeStruct((STREAMS, TOK,...]
where the time goes in v3:
time: 119 us
  Pallas kernels  119 us (100%)
    pallas_call x1, Pallas kernels, body(): pl.pallas_call(kernel, out_shape=(jax.ShapeDtypeStruct((STREAMS, TOK, COL...  114 us
    pallas_call x1, Pallas kernels, body(): pl.pallas_call(mix_kernel, out_shape=jax.ShapeDtypeStruct((STREAMS, TOK,...  4.85 us

profile of v3, /device:TPU:1, one launch (start us, length us, event | category | flops | bytes accessed | tf_op | source)
XLA Modules:
  0.0 119.1 jit_solution(8684405846655236206)
XLA Ops:
  0.0 114.2 %shard_map.82 = (f32[4,512,512]{2,1,0:T(8,128)}, f32[512,512]{1,0:T(8,128)}, f32[512,128]{1,0:T(8,128)}) custom-call(f32[4,512,512]{2,1,0:T(8,128)} %st_hbm.1, f32[24,4,512]{2,1,0:T(4,128)} %mw.1, f32[24]{0:T(128)} %bias.1, f32[3]{0:T(128)} %scale.1, bf16[32,128]{1,0:T(8,128)(2,1)} %bitcast.1, bf16[128,896]{1,0:T(8,128)(2,1)} %g_hbm.1, ...), custom_call_target="tpu_custom_call" | custom-call | tf_op jit(solution)/shard_map/pallas_call | solution.py:679
  114.2 4.8 %shard_map.83 = f32[4,512,512]{2,1,0:T(8,128)} custom-call(f32[4,512,512]{2,1,0:T(8,128)} %get-tuple-element.8.base_hbm, f32[512,512]{1,0:T(8,128)} %get-tuple-element.9.lo_hbm, f32[512,128]{1,0:T(8,128)} %get-tuple-element.10.post_hbm), custom_call_target="tpu_custom_call" | custom-call | tf_op jit(solution)/shard_map/pallas_call | solution.py:729

commit v4 on v3

--- a/solution.py
+++ b/solution.py
@@ -37,9 +37,9 @@
 
 
 def kernel(
-    st_hbm, mw, bias, scale, gain, g_hbm, u_hbm, d_hbm, base_hbm, lo_hbm, post_hbm,
+    st_hbm, mw_hbm, bias_hbm, scale_hbm, gain_hbm, g_hbm, u_hbm, d_hbm, base_hbm, lo_hbm, post_hbm,
     st, wg, wu, wd, xg, hid, rr, rl, sr, sl, pst, ost, sqx, pre_t, inv_t, tmp, g32,
-    base, lo, own, coef_t, loc_sem, out_sem, w_send, w_recv, ag_send, ag_recv, rs_send, rs_recv,
+    base, lo, own, coef_t, mw, bias, scale, gain, loc_sem, out_sem, w_send, w_recv, ag_send, ag_recv, rs_send, rs_recv,
     ps_send, ps_recv, os_send, os_recv, sq_send, sq_recv,
 ):
     s = lax.axis_index("seq")
@@ -69,14 +69,19 @@
         )
         for c in range(CHUNKS)
     ]
-    for c in w_copies + st_copies:
+    small = [
+        pltpu.make_async_copy(src, dst, loc_sem.at[CHUNKS + 3 + i])
+        for i, (src, dst) in enumerate(
+            ((mw_hbm, mw), (gain_hbm, gain), (scale_hbm, scale), (bias_hbm, bias))
+        )
+    ]
+    for c in w_copies + small + st_copies:
         c.start()
 
     barrier = pltpu.get_barrier_semaphore()
     peers = [x_up, x_dn, y_up, y_dn, other] + [z_peers[d] for d in range(1, NZ)]
     for peer in peers:
         pl.semaphore_signal(barrier, inc=1, device_id=peer, device_id_type=MESH)
-    g32[...] = gain[...].astype(F32)
     pl.semaphore_wait(barrier, len(peers))
 
     sends = []
@@ -249,6 +254,9 @@
         across_dn(i, 0)
 
     ones = jnp.ones((8, 128), F32)
+    for c in small:
+        c.wait()
+    g32[...] = gain[...].astype(F32)
 
     def ps_copy(c, d, owner):
         return remote(
@@ -515,11 +523,11 @@
     share_down(2, 1)
     gate_up(1, 4, 7)
     rs_step(0, 2, 4)
-    fwd_half_up(3)
-    fwd_half_dn(3)
     got_fwd_up(DOWN, 1)
     got_fwd_dn(DOWN, 1)
     share_down(2, 2)
+    fwd_half_up(3)
+    fwd_half_dn(3)
     down_shared(2)
     rs_step(1, 0, 4)
     got_half_up(3, 1)
@@ -588,7 +596,7 @@
                     v = wide[STREAMS * k] * src[0]
                     for j in range(1, STREAMS):
                         v = v + wide[STREAMS * k + j] * src[j]
-                    base[k, tok, lanes] = v
+                    base[k, tok, lanes] = v.astype(BF16)
             return carry
 
         lax.fori_loop(0, CT // rows, group, 0)
@@ -642,7 +650,7 @@
         lo_write(c).wait()
 
 
-def mix_kernel(base_hbm, lo_hbm, post_hbm, out_hbm, base, lo, post, in_sem, out_sem):
+def mix_kernel(base_hbm, lo_hbm, post_hbm, out_hbm, base, lo, post, out, in_sem, out_sem):
     def tokens(c):
         return pl.ds(c * MT, MT)
 
@@ -654,7 +662,7 @@
         )
 
     def write(c):
-        return pltpu.make_async_copy(base.at[:, tokens(c)], out_hbm.at[:, tokens(c)], out_sem.at[c])
+        return pltpu.make_async_copy(out.at[:, tokens(c)], out_hbm.at[:, tokens(c)], out_sem.at[c])
 
     for c in range(TOK // MT):
         for copy in reads(c):
@@ -664,7 +672,7 @@
             copy.wait()
         tok = slice(c * MT, (c + 1) * MT)
         for k in range(STREAMS):
-            base[k, tok, :] = base[k, tok, :] + post[tok, k : k + 1] * lo[tok, :]
+            out[k, tok, :] = base[k, tok, :].astype(F32) + post[tok, k : k + 1] * lo[tok, :]
         write(c).start()
     for c in range(TOK // MT):
         write(c).wait()
@@ -673,17 +681,15 @@
 def body(streams, mix_weight, mix_bias, mix_scale, norm_gain, gate_weight, up_weight, down_weight):
     gain = norm_gain.reshape(NZ * 4, 128)
     hbm = pl.BlockSpec(memory_space=pltpu.HBM)
-    vmem = pl.BlockSpec(memory_space=pltpu.VMEM)
-    smem = pl.BlockSpec(memory_space=pltpu.SMEM)
     dma = pltpu.SemaphoreType.DMA
     base, layer_out, post = pl.pallas_call(
         kernel,
         out_shape=(
-            jax.ShapeDtypeStruct((STREAMS, TOK, COLS), F32),
+            jax.ShapeDtypeStruct((STREAMS, TOK, COLS), BF16),
             jax.ShapeDtypeStruct((TOK, COLS), F32),
             jax.ShapeDtypeStruct((TOK, 128), F32),
         ),
-        in_specs=[hbm, vmem, smem, smem, vmem, hbm, hbm, hbm],
+        in_specs=[hbm] * 8,
         out_specs=(hbm, hbm, hbm),
         scratch_shapes=[
             pltpu.VMEM((STREAMS, TOK, COLS), F32),
@@ -703,11 +709,15 @@
             pltpu.VMEM((TOK, 128), F32),
             pltpu.VMEM((CT, COLS), F32),
             pltpu.VMEM((NZ * 4, 128), F32),
-            pltpu.VMEM((STREAMS, TOK, COLS), F32),
+            pltpu.VMEM((STREAMS, TOK, COLS), BF16),
             pltpu.VMEM((TOK, COLS), F32),
             pltpu.VMEM((TOK, COLS), F32),
             pltpu.VMEM((TOK, 128), F32),
-            dma((CHUNKS + 3,)),
+            pltpu.VMEM((6 * STREAMS, STREAMS, COLS), F32),
+            pltpu.SMEM((6 * STREAMS,), F32),
+            pltpu.SMEM((3,), F32),
+            pltpu.VMEM((NZ * 4, 128), BF16),
+            dma((CHUNKS + 7,)),
             dma((2 * CHUNKS + 1,)),
             dma((3, 36)),
             dma((3, 36)),
@@ -732,9 +742,10 @@
         in_specs=[hbm, hbm, hbm],
         out_specs=hbm,
         scratch_shapes=[
-            pltpu.VMEM((STREAMS, TOK, COLS), F32),
+            pltpu.VMEM((STREAMS, TOK, COLS), BF16),
             pltpu.VMEM((TOK, COLS), F32),
             pltpu.VMEM((TOK, 128), F32),
+            pltpu.VMEM((STREAMS, TOK, COLS), F32),
             dma((TOK // MT, 3)),
             dma((TOK // MT,)),
         ],

time: 119 us -> 117 us (0.983)
  Pallas kernels: 119 us -> 117 us
    pallas_call x1, Pallas kernels: 4.85 us -> 3.43 us  [body(): pl.pallas_call(mix_kernel, out_shape=jax.ShapeDtypeStruct((STREAMS, TOK,...]
where the time goes in v4:
time: 117 us
  Pallas kernels  117 us (100%)
    pallas_call x1, Pallas kernels, body(): pl.pallas_call(kernel, out_shape=(jax.ShapeDtypeStruct((STREAMS, TOK, COL...  113 us
    pallas_call x1, Pallas kernels, body(): pl.pallas_call(mix_kernel, out_shape=jax.ShapeDtypeStruct((STREAMS, TOK,...  3.43 us

profile of v4, /device:TPU:1, one launch (start us, length us, event | category | flops | bytes accessed | tf_op | source)
XLA Modules:
  0.0 116.7 jit_solution(6107582596855400164)
XLA Ops:
  0.0 113.3 %shard_map.82 = (bf16[4,512,512]{2,1,0:T(8,128)(2,1)}, f32[512,512]{1,0:T(8,128)}, f32[512,128]{1,0:T(8,128)}) custom-call(f32[4,512,512]{2,1,0:T(8,128)} %st_hbm.1, f32[24,4,512]{2,1,0:T(4,128)} %mw_hbm.1, f32[24]{0:T(128)} %bias_hbm.1, f32[3]{0:T(128)} %scale_hbm.1, bf16[32,128]{1,0:T(8,128)(2,1)} %bitcast.1, bf16[128,896]{1,0:T(8,128)(2,1)} %g_hbm.1, ...), custom_call_target="tpu_custom_call" | custom-call | tf_op jit(solution)/shard_map/pallas_call | solution.py:685
  113.3 3.4 %shard_map.83 = f32[4,512,512]{2,1,0:T(8,128)} custom-call(bf16[4,512,512]{2,1,0:T(8,128)(2,1)} %get-tuple-element.8.base_hbm, f32[512,512]{1,0:T(8,128)} %get-tuple-element.9.lo_hbm, f32[512,128]{1,0:T(8,128)} %get-tuple-element.10.post_hbm), custom_call_target="tpu_custom_call" | custom-call | tf_op jit(solution)/shard_map/pallas_call | solution.py:739

commit v5 on v4

--- a/solution.py
+++ b/solution.py
@@ -447,7 +447,7 @@
             hid[tok, lanes] = (g / (1.0 + jnp.exp(-g)) * u).astype(BF16)
             return carry
 
-        lax.fori_loop(first, last, tile, 0)
+        lax.fori_loop(first, last, tile, 0, unroll=True)
 
     def partial(dest, tok):
         a = hid[tok, :]
@@ -469,6 +469,40 @@
             device_id=right if q == 0 else left, device_id_type=MESH,
         )
 
+    def first_lanes(own):
+        return pl.ds(pl.multiple_of(256 * (core if own else 1 - core), 256), 256)
+
+    def first_copy(q, c, own):
+        src, dst = (sr, rr) if q == 0 else (sl, rl)
+        lanes = first_lanes(own)
+        k = 0 if own else 4
+        return pltpu.make_async_remote_copy(
+            src_ref=src.at[c, 0, :, lanes], dst_ref=dst.at[c, 0, :, lanes],
+            send_sem=rs_send.at[q, c, k], recv_sem=rs_recv.at[q, c, k],
+            device_id=right if q == 0 else left, device_id_type=MESH,
+        )
+
+    def rs_first(own, first, last):
+        def chunk(c, carry):
+            odd = lax.rem(c, 2)
+            tok = pl.ds(pl.multiple_of(c * CT, CT), CT)
+            for q in range(2):
+                n_hops = 4 - odd if q == 0 else 3 + odd
+                dest = wrap(z + n_hops, NZ) if q == 0 else wrap(z - n_hops, NZ)
+                src = sr if q == 0 else sl
+                j = 2 * lax.rem(dest, 2)
+                cc = core if own else 1 - core
+                b0 = wd[cc, lax.div(dest, 2), j]
+                b1 = wd[cc, lax.div(dest, 2), j + 1]
+                p = jnp.dot(
+                    hid[tok, :], jnp.concatenate([b0, b1], axis=1), preferred_element_type=F32
+                )
+                src[c, 0, :, first_lanes(own)] = p.astype(BF16)
+                first_copy(q, c, own).start()
+            return carry
+
+        lax.fori_loop(first, last, chunk, 0)
+
     def rs_step(t, first, last):
         def chunk(c, carry):
             odd = lax.rem(c, 2)
@@ -486,7 +520,11 @@
                     else:
                         tmp[:, 0:256] = p0
                         tmp[:, 256:512] = p1
-                        rs_copy(q, c, t - 1).wait_recv()
+                        if t == 1 and first < 2:
+                            first_copy(q, c, True).wait_recv()
+                            first_copy(q, c, False).wait_recv()
+                        else:
+                            rs_copy(q, c, t - 1).wait_recv()
                         src[c, t] = (tmp[...] + dst[c, t - 1].astype(F32)).astype(BF16)
                     rs_copy(q, c, t).start()
 
@@ -504,32 +542,34 @@
     got_dn(DOWN, 0)
     share_down(0, 1)
     ag_step(3, (2, 3))
+    gate_up(1, 0, 1)
     got_fwd_up(DOWN, 0)
     share_down(0, 2)
     got_fwd_dn(DOWN, 0)
     share_down(1, 2)
-    gate_up(1, 0, 1)
+    rs_first(True, 0, 2)
+    gate_up(1, 1, 3)
     shared(DOWN, 18, own_down)
     down_shared(0)
     down_shared(1)
-    rs_step(0, 0, 2)
+    rs_first(False, 0, 2)
     fwd_half_up(2)
     fwd_half_dn(2)
     send_halves(3)
-    gate_up(1, 1, 4)
+    gate_up(1, 3, 7)
+    rs_step(0, 2, 4)
     got_half_up(2, 1)
     share_down(2, 0)
     got_half_dn(2, 0)
     share_down(2, 1)
-    gate_up(1, 4, 7)
-    rs_step(0, 2, 4)
     got_fwd_up(DOWN, 1)
     got_fwd_dn(DOWN, 1)
     share_down(2, 2)
+    down_shared(2)
+    rs_step(1, 0, 2)
     fwd_half_up(3)
     fwd_half_dn(3)
-    down_shared(2)
-    rs_step(1, 0, 4)
+    rs_step(1, 2, 4)
     got_half_up(3, 1)
     share_down(3, 0)
     got_half_dn(3, 0)
@@ -643,7 +683,11 @@
     for c in range(CHUNKS):
         for q in range(2):
             for t in range(hops(c, q == 0)):
-                rs_copy(q, c, t).wait_send()
+                if t == 0 and c < 2:
+                    first_copy(q, c, True).wait_send()
+                    first_copy(q, c, False).wait_send()
+                else:
+                    rs_copy(q, c, t).wait_send()
     post_write().wait()
     for c in range(CHUNKS):
         base_write(c).wait()
@@ -723,8 +767,8 @@
             dma((3, 36)),
             dma((2, CHUNKS, 4)),
             dma((2, CHUNKS, 4)),
-            dma((2, CHUNKS, 4)),
-            dma((2, CHUNKS, 4)),
+            dma((2, CHUNKS, 5)),
+            dma((2, CHUNKS, 5)),
             dma((CHUNKS, 8)),
             dma((CHUNKS, 8)),
             dma((8,)),

time: 117 us -> 114 us (0.974)
  Pallas kernels: 117 us -> 113 us
    pallas_call x1, Pallas kernels: 113 us -> 110 us  [body(): pl.pallas_call(kernel, out_shape=(jax.ShapeDtypeStruct((STREAMS, TOK, COL...]
where the time goes in v5:
time: 114 us
  Pallas kernels  113 us (99%)
    pallas_call x1, Pallas kernels, body(): pl.pallas_call(kernel, out_shape=(jax.ShapeDtypeStruct((STREAMS, TOK, COL...  110 us
    pallas_call x1, Pallas kernels, body(): pl.pallas_call(mix_kernel, out_shape=jax.ShapeDtypeStruct((STREAMS, TOK,...  3.43 us

profile of v5, /device:TPU:1, one launch (start us, length us, event | category | flops | bytes accessed | tf_op | source)
XLA Modules:
  0.0 113.7 jit_solution(14496771645204878811)
XLA Ops:
  0.0 110.1 %shard_map.82 = (bf16[4,512,512]{2,1,0:T(8,128)(2,1)}, f32[512,512]{1,0:T(8,128)}, f32[512,128]{1,0:T(8,128)}) custom-call(f32[4,512,512]{2,1,0:T(8,128)} %st_hbm.1, f32[24,4,512]{2,1,0:T(4,128)} %mw_hbm.1, f32[24]{0:T(128)} %bias_hbm.1, f32[3]{0:T(128)} %scale_hbm.1, bf16[32,128]{1,0:T(8,128)(2,1)} %bitcast.1, bf16[128,896]{1,0:T(8,128)(2,1)} %g_hbm.1, ...), custom_call_target="tpu_custom_call" | custom-call | tf_op jit(solution)/shard_map/pallas_call | solution.py:729
  110.1 3.4 %shard_map.83 = f32[4,512,512]{2,1,0:T(8,128)} custom-call(bf16[4,512,512]{2,1,0:T(8,128)(2,1)} %get-tuple-element.8.base_hbm, f32[512,512]{1,0:T(8,128)} %get-tuple-element.9.lo_hbm, f32[512,128]{1,0:T(8,128)} %get-tuple-element.10.post_hbm), custom_call_target="tpu_custom_call" | custom-call | tf_op jit(solution)/shard_map/pallas_call | solution.py:783

commit v6 on v5

--- a/solution.py
+++ b/solution.py
@@ -482,26 +482,26 @@
             device_id=right if q == 0 else left, device_id_type=MESH,
         )
 
-    def rs_first(own, first, last):
-        def chunk(c, carry):
-            odd = lax.rem(c, 2)
-            tok = pl.ds(pl.multiple_of(c * CT, CT), CT)
-            for q in range(2):
-                n_hops = 4 - odd if q == 0 else 3 + odd
-                dest = wrap(z + n_hops, NZ) if q == 0 else wrap(z - n_hops, NZ)
-                src = sr if q == 0 else sl
-                j = 2 * lax.rem(dest, 2)
-                cc = core if own else 1 - core
-                b0 = wd[cc, lax.div(dest, 2), j]
-                b1 = wd[cc, lax.div(dest, 2), j + 1]
-                p = jnp.dot(
-                    hid[tok, :], jnp.concatenate([b0, b1], axis=1), preferred_element_type=F32
-                )
-                src[c, 0, :, first_lanes(own)] = p.astype(BF16)
-                first_copy(q, c, own).start()
-            return carry
-
-        lax.fori_loop(first, last, chunk, 0)
+    def rs_first(own):
+        cc = core if own else 1 - core
+        lanes = first_lanes(own)
+
+        def product(dest, tok):
+            j = 2 * lax.rem(dest, 2)
+            b0 = wd[cc, lax.div(dest, 2), j]
+            b1 = wd[cc, lax.div(dest, 2), j + 1]
+            both = jnp.concatenate([b0, b1], axis=1)
+            return jnp.dot(hid[tok, :], both, preferred_element_type=F32).astype(BF16)
+
+        far = product(wrap(z + 4, NZ), slice(0, 2 * CT))
+        sr[0, 0, :, lanes] = far[:CT]
+        sl[1, 0, :, lanes] = far[CT:]
+        first_copy(0, 0, own).start()
+        first_copy(1, 1, own).start()
+        sl[0, 0, :, lanes] = product(wrap(z - 3, NZ), slice(0, CT))
+        first_copy(1, 0, own).start()
+        sr[1, 0, :, lanes] = product(wrap(z + 3, NZ), slice(CT, 2 * CT))
+        first_copy(0, 1, own).start()
 
     def rs_step(t, first, last):
         def chunk(c, carry):
@@ -547,12 +547,12 @@
     share_down(0, 2)
     got_fwd_dn(DOWN, 0)
     share_down(1, 2)
-    rs_first(True, 0, 2)
+    rs_first(True)
     gate_up(1, 1, 3)
     shared(DOWN, 18, own_down)
     down_shared(0)
     down_shared(1)
-    rs_first(False, 0, 2)
+    rs_first(False)
     fwd_half_up(2)
     fwd_half_dn(2)
     send_halves(3)

time: 114 us -> 114 us (level)
  no operation moved by 1% of the time
where the time goes in v6:
time: 114 us
  Pallas kernels  114 us (100%)
    pallas_call x1, Pallas kernels, body(): pl.pallas_call(kernel, out_shape=(jax.ShapeDtypeStruct((STREAMS, TOK, COL...  110 us
    pallas_call x1, Pallas kernels, body(): pl.pallas_call(mix_kernel, out_shape=jax.ShapeDtypeStruct((STREAMS, TOK,...  3.43 us

profile of v6, /device:TPU:1, one launch (start us, length us, event | category | flops | bytes accessed | tf_op | source)
XLA Modules:
  0.0 113.7 jit_solution(3522504667961066634)
XLA Ops:
  0.0 110.1 %shard_map.82 = (bf16[4,512,512]{2,1,0:T(8,128)(2,1)}, f32[512,512]{1,0:T(8,128)}, f32[512,128]{1,0:T(8,128)}) custom-call(f32[4,512,512]{2,1,0:T(8,128)} %st_hbm.1, f32[24,4,512]{2,1,0:T(4,128)} %mw_hbm.1, f32[24]{0:T(128)} %bias_hbm.1, f32[3]{0:T(128)} %scale_hbm.1, bf16[32,128]{1,0:T(8,128)(2,1)} %bitcast.1, bf16[128,896]{1,0:T(8,128)(2,1)} %g_hbm.1, ...), custom_call_target="tpu_custom_call" | custom-call | tf_op jit(solution)/shard_map/pallas_call | solution.py:729
  110.1 3.4 %shard_map.83 = f32[4,512,512]{2,1,0:T(8,128)} custom-call(bf16[4,512,512]{2,1,0:T(8,128)(2,1)} %get-tuple-element.8.base_hbm, f32[512,512]{1,0:T(8,128)} %get-tuple-element.9.lo_hbm, f32[512,128]{1,0:T(8,128)} %get-tuple-element.10.post_hbm), custom_call_target="tpu_custom_call" | custom-call | tf_op jit(solution)/shard_map/pallas_call | solution.py:783
